TPU v7x, 32 devices: a whole 2x2x4 slice. The times are simulated.
32 devices in a mesh: shard: 8 (over z, x), width: 4 (over y, core).
Axes of the slice: x: 2, y: 2, z: 4, core: 2. Of those that a mesh axis runs over, the one named last changes fastest.
Arguments:
- w_query: float32 [4096, 4096], P('shard', 'width'), may hold values from -0.125 to 0.125
- first_query: float32 [4096, 4096], P('shard', 'width'), may hold values from -0.09375 to 0.09375
- second_query: float32 [4096, 4096], P('shard', 'width'), may hold values from -0.09375 to 0.09375
- w_key: float32 [4096, 1024], P('shard', 'width'), may hold values from -0.125 to 0.125
- first_key: float32 [4096, 1024], P('shard', 'width'), may hold values from -0.09375 to 0.09375
- second_key: float32 [4096, 1024], P('shard', 'width'), may hold values from -0.09375 to 0.09375
- w_value: float32 [4096, 1024], P('shard', 'width'), may hold values from -0.125 to 0.125
- first_value: float32 [4096, 1024], P('shard', 'width'), may hold values from -0.09375 to 0.09375
- second_value: float32 [4096, 1024], P('shard', 'width'), may hold values from -0.09375 to 0.09375
- norm_train: float32 [4096], P(('shard', 'width')), may hold values from 0.25 to 1.75
- norm_step: float32 [4096], P(('shard', 'width')), may hold values from -0.3 to 0.3
Outputs:
- serving_query: bfloat16 [4096, 4096], P(None, 'width')
- serving_key: bfloat16 [4096, 1024], P(None, 'width')
- serving_value: bfloat16 [4096, 1024], P(None, 'width')
- column_query: float32 [4096], P('width')
- column_key: float32 [1024], P('width')
- column_value: float32 [1024], P('width')
- serve_norm: bfloat16 [4096], replicated
- whole_query: float32 [4096, 4096], P('shard', 'width')
- whole_key: float32 [4096, 1024], P('shard', 'width')
- whole_value: float32 [4096, 1024], P('shard', 'width')
All inputs are finite; a program needn't handle non-finite values. Where the computation divides by a largest or mean magnitude, that divisor is 1e-20 or more.
Results may differ from a plain program's by a relative error of at most 0.0004.
Values may be sent and summed in bfloat16 or wider, within the bound.
A program may use at most 128 MiB of HBM per device.

v0:
```python
import functools

import jax
import jax.numpy as jnp
from jax import lax
from jax.experimental import pallas as pl
from jax.experimental.pallas import tpu as pltpu
from jax.sharding import PartitionSpec as P

learn_rate = 0.2
hold_rate = 0.8
MESH = pl.DeviceIdType.MESH
TILE = 16


def gather_kernel(
    n,
    width,
    w_q,
    w_k,
    w_v,
    norm_in,
    out_q,
    out_k,
    out_v,
    col_q,
    col_k,
    col_v,
    norm_out,
    sums,
    sum_send,
    sum_recv,
    wid_send,
    wid_recv,
    nrm_send,
    nrm_recv,
    z_send,
    z_recv,
    x_send,
    x_recv,
):
    me = lax.axis_index("shard")
    me_w = lax.axis_index("width")
    depth = n // 2
    z, x = lax.div(me, 2), lax.rem(me, 2)
    rows = w_q.shape[0]
    ins, outs, cols = (w_q, w_k, w_v), (out_q, out_k, out_v), (col_q, col_k, col_v)
    extents = [ref.shape[1] for ref in ins]
    starts = [sum(extents[:i]) for i in range(3)]

    barrier = pltpu.get_barrier_semaphore()
    for k in range(1, n):
        pl.semaphore_signal(
            barrier, inc=1, device_id={"shard": lax.rem(me + k, n)}, device_id_type=MESH
        )
    for k in range(1, width):
        pl.semaphore_signal(
            barrier, inc=1, device_id={"width": lax.rem(me_w + k, width)}, device_id_type=MESH
        )

    for ref, start, extent in zip(ins, starts, extents):

        def add(i, total, ref=ref):
            for j in range(4):
                total = total + jnp.abs(ref[pl.ds(pl.multiple_of(i * 32 + j * 8, 8), 8), :])
            return total

        total = lax.fori_loop(0, rows // 32, add, jnp.zeros((8, extent), jnp.float32))
        sums[me, :, start : start + extent] = jnp.sum(total, axis=0, keepdims=True)
    norm_out[me, me_w] = norm_in[...]

    pl.semaphore_wait(barrier, n - 1 + width - 1)

    sum_copies = []
    for k in range(1, n):
        copy = pltpu.make_async_remote_copy(
            src_ref=sums.at[me],
            dst_ref=sums.at[me],
            send_sem=sum_send.at[k - 1],
            recv_sem=sum_recv.at[k - 1],
            device_id={"shard": lax.rem(me + k, n)},
            device_id_type=MESH,
        )
        copy.start()
        sum_copies.append(copy)
    wid_copies = []
    for k in range(1, width):
        copy = pltpu.make_async_remote_copy(
            src_ref=norm_in,
            dst_ref=norm_out.at[me, me_w],
            send_sem=wid_send.at[k - 1],
            recv_sem=wid_recv.at[k - 1],
            device_id={"width": lax.rem(me_w + k, width)},
            device_id_type=MESH,
        )
        copy.start()
        wid_copies.append(copy)
    for copy in sum_copies:
        copy.wait_recv()

    for ref, out, col, start, extent in zip(ins, outs, cols, starts, extents):
        total = sums[0, :, start : start + extent]
        for k in range(1, n):
            total = total + sums[k, :, start : start + extent]
        col[...] = total / (rows * n)

    for ref, out, col in zip(ins, outs, cols):
        scale = col[...]

        def narrow(i, carry, ref=ref, out=out, scale=scale):
            here = pl.multiple_of(i * TILE, TILE)
            there = pl.multiple_of(me * rows + i * TILE, TILE)
            out[pl.ds(there, TILE), :] = (ref[pl.ds(here, TILE), :] / scale).astype(jnp.bfloat16)
            return carry

        lax.fori_loop(0, rows // TILE, narrow, 0)

    part_g = TILE * max(1, round(rows * 4 / 9 / (2 * TILE)))
    part_h = rows // 2 - part_g
    g_at = (0, part_g)
    h_at = (2 * part_g, 2 * part_g + part_h)
    started = []

    def send(owner, at, size, target, send_sems, recv_sems):
        copies = []
        where = pl.ds(pl.multiple_of(owner * rows + at, TILE), size)
        for i, out in enumerate(outs):
            copy = pltpu.make_async_remote_copy(
                src_ref=out.at[where],
                dst_ref=out.at[where],
                send_sem=send_sems.at[i],
                recv_sem=recv_sems.at[i],
                device_id={"shard": target},
                device_id_type=MESH,
            )
            copy.start()
            copies.append(copy)
        started.extend(copies)
        return copies

    def arrived(copies):
        for copy in copies:
            copy.wait_recv()

    other = z * 2 + 1 - x
    step_of = (1, depth - 1)
    next_of = [lax.rem(z + step_of[d], depth) * 2 + x for d in range(2)]

    def ring_send(kind, d, s):
        at_z = lax.rem(z + s * step_of[1 - d], depth)
        column = 1 - x if kind == 2 else x
        at, size = ((g_at[d], part_g), (h_at[d], part_h), (h_at[d], part_h))[kind]
        return send(
            at_z * 2 + column,
            at,
            size,
            next_of[d],
            z_send.at[d, kind, s],
            z_recv.at[d, kind, s],
        )

    def x_own(unit):
        at, size = ((h_at[0], part_h), (h_at[1], part_h), (g_at[0], part_g), (g_at[1], part_g))[unit]
        return send(me, at, size, other, x_send.at[unit], x_recv.at[unit])

    def x_forward(d, s):
        at_z = lax.rem(z + (s + 1) * step_of[1 - d], depth)
        unit = 4 + 2 * s + d
        return send(at_z * 2 + x, g_at[d], part_g, other, x_send.at[unit], x_recv.at[unit])

    ring = {}
    crossed = [x_own(0)]
    for d in range(2):
        ring[0, d, 0] = ring_send(0, d, 0)
    crossed.append(x_own(1))
    for d in range(2):
        ring[1, d, 0] = ring_send(1, d, 0)
    crossed.append(x_own(2))
    crossed.append(x_own(3))

    for copy in wid_copies:
        copy.wait_recv()
    nrm_copies = []
    for k in range(1, n):
        copy = pltpu.make_async_remote_copy(
            src_ref=norm_out.at[me],
            dst_ref=norm_out.at[me],
            send_sem=nrm_send.at[k - 1],
            recv_sem=nrm_recv.at[k - 1],
            device_id={"shard": lax.rem(me + k, n)},
            device_id_type=MESH,
        )
        copy.start()
        nrm_copies.append(copy)

    def ring_arrival(kind, s):
        for d in range(2):
            arrived(ring[kind, d, s])
            if s + 1 < depth - 1:
                ring[kind, d, s + 1] = ring_send(kind, d, s + 1)
            if kind == 0:
                crossed.append(x_forward(d, s))

    def cross_arrival(d):
        arrived(crossed[d])
        ring[2, d, 0] = ring_send(2, d, 0)

    ring_arrival(0, 0)
    cross_arrival(0)
    ring_arrival(1, 0)
    cross_arrival(1)
    for s in range(1, depth - 1):
        ring_arrival(0, s)
        ring_arrival(2, s - 1)
        ring_arrival(1, s)
    ring_arrival(2, depth - 2)
    for copies in crossed[2:]:
        arrived(copies)
    for copy in nrm_copies:
        copy.wait_recv()
    for copy in sum_copies + wid_copies + nrm_copies + started:
        copy.wait_send()


def local(
    n,
    width,
    w_query,
    first_query,
    second_query,
    w_key,
    first_key,
    second_key,
    w_value,
    first_value,
    second_value,
    norm_train,
    norm_step,
):
    whole_query = w_query - learn_rate * (hold_rate * first_query + second_query)
    whole_key = w_key - learn_rate * (hold_rate * first_key + second_key)
    whole_value = w_value - learn_rate * (hold_rate * first_value + second_value)
    norm = (norm_train + norm_step).reshape(1, -1)
    wholes = (whole_query, whole_key, whole_value)
    rows = whole_query.shape[0]
    extents = [each.shape[1] for each in wholes]
    piece = norm.shape[1]
    depth = n // 2
    dma = pltpu.SemaphoreType.DMA
    vmem = pl.BlockSpec(memory_space=pltpu.VMEM)
    gathered = pl.pallas_call(
        functools.partial(gather_kernel, n, width),
        out_shape=[jax.ShapeDtypeStruct((rows * n, e), jnp.bfloat16) for e in extents]
        + [jax.ShapeDtypeStruct((1, e), jnp.float32) for e in extents]
        + [jax.ShapeDtypeStruct((n, width, 1, piece), jnp.float32)],
        in_specs=[vmem] * 4,
        out_specs=[vmem] * 7,
        scratch_shapes=[
            pltpu.VMEM((n, 1, sum(extents)), jnp.float32),
            dma((n - 1,)),
            dma((n - 1,)),
            dma((width - 1,)),
            dma((width - 1,)),
            dma((n - 1,)),
            dma((n - 1,)),
            dma((2, 3, depth - 1, 3)),
            dma((2, 3, depth - 1, 3)),
            dma((4 + 2 * (depth - 1), 3)),
            dma((4 + 2 * (depth - 1), 3)),
        ],
        compiler_params=pltpu.CompilerParams(
            collective_id=0, has_side_effects=True, vmem_limit_bytes=48 * 1024 * 1024
        ),
    )(*wholes, norm)
    serving_query, serving_key, serving_value, column_query, column_key, column_value, gain = gathered
    return (
        serving_query,
        serving_key,
        serving_value,
        column_query.reshape(-1),
        column_key.reshape(-1),
        column_value.reshape(-1),
        gain.reshape(-1).astype(jnp.bfloat16),
        whole_query,
        whole_key,
        whole_value,
    )


def solution(mesh):
    split = P("shard", "width")
    both = P(("shard", "width"))
    n, width = mesh.shape["shard"], mesh.shape["width"]
    return jax.shard_map(
        functools.partial(local, n, width),
        mesh=mesh,
        in_specs=(split,) * 9 + (both, both),
        out_specs=(P(None, "width"),) * 3 + (P("width"),) * 3 + (P(),) + (split,) * 3,
        check_vma=False,
    )
```

profile of v0, /device:TPU:0, one launch (start us, length us, event | category | flops | bytes accessed | tf_op | source)
XLA Modules:
  0.0 196.8 jit_solution(2994617729672698503)
XLA Ops:
  0.6 0.7 add_bitcast_fusion.norm_in
  1.3 0.0 copy-start.2
  1.3 0.0 copy-start.3
  1.3 2.2 %multiply_subtract_fusion.1 = (f32[512,256]{1,0:T(8,128)S(1)}, f32[512,256]{1,0:T(8,128)S(1)}) fusion(f32[512,256]{1,0:T(8,128)} %param.17, f32[512,256]{1,0:T(8,128)} %param.19, f32[512,256]{1,0:T(8,128)} %param.18, f32[512,256]{1,0:T(8,128)} %param.14, f32[512,256]{1,0:T(8,128)} %param.16, f32[512,256]{1,0:T(8,128)} %param.15), kind=kLoop, calls=%fused_computation.1 | loop fusion | flops 1048576 | bytes 4194304 | tf_op jit(solution)/shard_map/sub | solution.py:242
  3.5 0.0 copy-start
  3.5 0.0 copy-start.1
  3.5 0.3 copy-done.2
  3.9 0.6 copy-done.3
  4.5 3.4 %multiply_subtract_fusion.w_q = f32[512,1024]{1,0:T(8,128)} fusion(f32[512,1024]{1,0:T(8,128)S(1)} %copy-done.2, f32[512,1024]{1,0:T(8,128)S(1)} %copy-done.3, f32[512,1024]{1,0:T(8,128)} %param.12), kind=kLoop, calls=%fused_computation | loop fusion | flops 2097152 | bytes 8388608 | tf_op jit(solution)/shard_map/sub | solution.py:240
  7.9 0.0 copy-done
  7.9 0.0 copy-done.1
  7.9 176.1 %shard_map.186 = (bf16[4096,1024]{1,0:T(8,128)(2,1)}, bf16[4096,256]{1,0:T(8,128)(2,1)S(1)}, bf16[4096,256]{1,0:T(8,128)(2,1)S(1)}, f32[1,1024]{1,0:T(1,128)S(1)...) custom-call(f32[512,1024]{1,0:T(8,128)} %multiply_subtract_fusion.w_q, ...), custom_call_target="tpu_custom_call" | custom-call | tf_op jit(solution)/shard_map/pallas_call | solution.py:251
  184.1 0.6 convert_reduce_fusion
  184.7 7.8 %copy.27 = bf16[4096,1024]{1,0:T(8,128)(2,1)} copy(bf16[4096,1024]{1,0:T(8,128)(2,1)} %get-tuple-element.36) | data formatting | bytes 16777216
  192.5 1.3 copy.28
  193.8 1.3 copy.29
  195.1 0.6 copy.30
  195.7 0.6 copy.31
  196.3 0.6 copy.32
Async XLA Ops:
  1.3 2.5 %copy-start.2 = (f32[512,1024]{1,0:T(8,128)S(1)}, f32[512,1024]{1,0:T(8,128)}, u32[]{:S(2)}) copy-start(f32[512,1024]{1,0:T(8,128)} %param.11) | copy-start | bytes 6291460
  1.3 3.2 %copy-start.3 = (f32[512,1024]{1,0:T(8,128)S(1)}, f32[512,1024]{1,0:T(8,128)}, u32[]{:S(2)}) copy-start(f32[512,1024]{1,0:T(8,128)} %param.13) | copy-start | bytes 6291460
  3.5 4.4 %copy-start = (f32[512,256]{1,0:T(8,128)}, f32[512,256]{1,0:T(8,128)S(1)}, u32[]{:S(2)}) copy-start(f32[512,256]{1,0:T(8,128)S(1)} %get-tuple-element.45.w_v) | copy-start | bytes 1572868
  3.5 4.4 %copy-start.1 = (f32[512,256]{1,0:T(8,128)}, f32[512,256]{1,0:T(8,128)S(1)}, u32[]{:S(2)}) copy-start(f32[512,256]{1,0:T(8,128)S(1)} %get-tuple-element.44.w_k) | copy-start | bytes 1572868
where the time goes:
time: 197 us
  Pallas kernels  176 us (89%)
  local copies, waits for them, and re-layouts  13.1 us (7%)
  other arithmetic  6.96 us (4%)
    pallas_call x1, Pallas kernels, local(): pl.pallas_call(functools.partial(gather_kernel, n, width), out_shape=[jax...  176 us
    unnamed x14, local copies, waits for them, and re-layouts  13.1 us

commit v1 on v0

v1 whole, which is shorter than its diff:
```python
import functools

import jax
import jax.numpy as jnp
from jax import lax
from jax.experimental import pallas as pl
from jax.experimental.pallas import tpu as pltpu
from jax.sharding import PartitionSpec as P

learn_rate = 0.2
hold_rate = 0.8
MESH = pl.DeviceIdType.MESH
TILE = 16
DOWN, UP, CROSS = 0, 1, 2


def plan_units(rows, extents):
    least = min(extents)
    units = []
    for i in sorted(range(len(extents)), key=lambda i: extents[i]):
        count = max(1, min(extents[i] // least, rows // TILE))
        size = rows // count
        units += [(i, j * size, size) for j in range(count)]
    return units


def gather_kernel(
    n,
    width,
    units,
    w_q,
    first_q,
    second_q,
    w_k,
    first_k,
    second_k,
    w_v,
    first_v,
    second_v,
    norm_train,
    norm_step,
    out_q,
    out_k,
    out_v,
    whole_q,
    whole_k,
    whole_v,
    col_q,
    col_k,
    col_v,
    norm_out,
    in_q,
    in_k,
    in_v,
    sums_q,
    sums_k,
    sums_v,
    in_norm,
    norm_sem,
    load_sem,
    sum_send,
    sum_recv,
    wid_send,
    wid_recv,
    nrm_send,
    nrm_recv,
    link_send,
    link_recv,
):
    me = lax.axis_index("shard")
    me_w = lax.axis_index("width")
    depth = n // 2
    z, x = lax.div(me, 2), lax.rem(me, 2)
    count = len(units)
    half = count // 2
    outs, wholes, cols = (out_q, out_k, out_v), (whole_q, whole_k, whole_v), (col_q, col_k, col_v)
    stages, sums = (in_q, in_k, in_v), (sums_q, sums_k, sums_v)
    sources = ((w_q, first_q, second_q), (w_k, first_k, second_k), (w_v, first_v, second_v))
    rows = whole_q.shape[0]
    order = list(dict.fromkeys(unit[0] for unit in units))

    barrier = pltpu.get_barrier_semaphore()
    for k in range(1, n):
        pl.semaphore_signal(
            barrier, inc=1, device_id={"shard": lax.rem(me + k, n)}, device_id_type=MESH
        )
    for k in range(1, width):
        pl.semaphore_signal(
            barrier, inc=1, device_id={"width": lax.rem(me_w + k, width)}, device_id_type=MESH
        )

    loads = []
    for u, (i, at, size) in enumerate(units):
        group = []
        for j in range(3):
            copy = pltpu.make_async_copy(
                sources[i][j].at[pl.ds(at, size)], stages[i].at[j, pl.ds(at, size)], load_sem.at[u, j]
            )
            copy.start()
            group.append(copy)
        loads.append(group)
    norm_loads = [
        pltpu.make_async_copy(ref, in_norm.at[j], norm_sem.at[j])
        for j, ref in enumerate((norm_train, norm_step))
    ]
    for copy in norm_loads:
        copy.start()

    sum_copies = {}
    wid_copies = []
    met = False
    for i in order:
        stage, whole = stages[i], wholes[i]
        total = jnp.zeros((8, whole.shape[1]), jnp.float32)
        for u, (owner, at, size) in enumerate(units):
            if owner != i:
                continue
            for copy in loads[u]:
                copy.wait()

            def update(r, total, at=at, stage=stage, whole=whole):
                for j in range(TILE // 8):
                    here = pl.ds(pl.multiple_of(at + r * TILE + j * 8, 8), 8)
                    new = stage[0, here] - learn_rate * (hold_rate * stage[1, here] + stage[2, here])
                    whole[here, :] = new
                    total = total + jnp.abs(new)
                return total

            total = lax.fori_loop(0, size // TILE, update, total)
        sums[i][me] = jnp.sum(total, axis=0, keepdims=True)
        if not met:
            for copy in norm_loads:
                copy.wait()
            norm_out[me, me_w] = in_norm[0] + in_norm[1]
            pl.semaphore_wait(barrier, n - 1 + width - 1)
        sum_copies[i] = []
        for k in range(1, n):
            copy = pltpu.make_async_remote_copy(
                src_ref=sums[i].at[me],
                dst_ref=sums[i].at[me],
                send_sem=sum_send.at[i, k - 1],
                recv_sem=sum_recv.at[i, k - 1],
                device_id={"shard": lax.rem(me + k, n)},
                device_id_type=MESH,
            )
            copy.start()
            sum_copies[i].append(copy)
        if not met:
            for k in range(1, width):
                copy = pltpu.make_async_remote_copy(
                    src_ref=norm_out.at[me, me_w],
                    dst_ref=norm_out.at[me, me_w],
                    send_sem=wid_send.at[k - 1],
                    recv_sem=wid_recv.at[k - 1],
                    device_id={"width": lax.rem(me_w + k, width)},
                    device_id_type=MESH,
                )
                copy.start()
                wid_copies.append(copy)
        met = True

    targets = (lax.max(z - 1, 0) * 2 + x, lax.min(z + 1, depth - 1) * 2 + x, z * 2 + 1 - x)

    def piece(owner, u, way, slot):
        i, at, size = units[u]
        where = pl.ds(pl.multiple_of(owner * rows + at, TILE), size)
        return pltpu.make_async_remote_copy(
            src_ref=outs[i].at[where],
            dst_ref=outs[i].at[where],
            send_sem=link_send.at[way, slot, u],
            recv_sem=link_recv.at[way, slot, u],
            device_id={"shard": targets[way]},
            device_id_type=MESH,
        )

    def crosses(source, u):
        low = (z >= 1) & (z < depth // 2) & (source == z - 1)
        high = (z >= depth // 2) & (z <= depth - 2) & (source == z + 1)
        no = low | high
        if u >= half:
            no = no | ((z == 0) & (source == depth - 1)) | ((z == depth - 1) & (source == 0))
        return jnp.logical_not(no)

    def send(owner_z, column, u, way, slot):
        piece(owner_z * 2 + column, u, way, slot).start()

    for i in order:
        for copy in sum_copies[i]:
            copy.wait_recv()
        total = sums[i][0]
        for k in range(1, n):
            total = total + sums[i][k]
        col = total / (rows * n)
        cols[i][...] = col
        factor = jnp.broadcast_to(1.0 / col, (TILE, col.shape[1]))
        whole, out = wholes[i], outs[i]
        for u, (owner, at, size) in enumerate(units):
            if owner != i:
                continue

            def narrow(r, carry, at=at, whole=whole, out=out, factor=factor):
                here = pl.multiple_of(at + r * TILE, TILE)
                there = pl.multiple_of(me * rows + at + r * TILE, TILE)
                out[pl.ds(there, TILE), :] = (whole[pl.ds(here, TILE), :] * factor).astype(jnp.bfloat16)
                return carry

            lax.fori_loop(0, size // TILE, narrow, 0)

            @pl.when(z >= 1)
            def _(u=u):
                send(z, x, u, DOWN, 0)

            @pl.when(z <= depth - 2)
            def _(u=u):
                send(z, x, u, UP, 0)

            send(z, x, u, CROSS, 0)

    for copy in wid_copies:
        copy.wait_recv()
    nrm_copies = []
    for k in range(1, n):
        copy = pltpu.make_async_remote_copy(
            src_ref=norm_out.at[me],
            dst_ref=norm_out.at[me],
            send_sem=nrm_send.at[k - 1],
            recv_sem=nrm_recv.at[k - 1],
            device_id={"shard": lax.rem(me + k, n)},
            device_id_type=MESH,
        )
        copy.start()
        nrm_copies.append(copy)

    last = depth - 1
    low_end, high_end = z <= depth // 2 - 2, z >= depth // 2 + 1

    def step(t, carry):
        for u in range(count):

            @pl.when(z + t <= last)
            def _(u=u):
                piece(me, u, DOWN, t - 1).wait_recv()

                @pl.when(z >= 1)
                def _():
                    send(z + t, x, u, DOWN, t)

                @pl.when(crosses(z + t, u))
                def _():
                    send(z + t, x, u, CROSS, t)

            @pl.when(z - t >= 0)
            def _(u=u):
                piece(me, u, UP, t - 1).wait_recv()

                @pl.when(z <= depth - 2)
                def _():
                    send(z - t, x, u, UP, t)

                @pl.when(crosses(z - t, u))
                def _():
                    send(z - t, x, u, CROSS, depth - t)

            @pl.when((t == 1) & (low_end | high_end))
            def _(u=u):
                piece(me, u, CROSS, 0).wait_recv()

                @pl.when(low_end)
                def _():
                    send(z, 1 - x, u, UP, last)

                @pl.when(high_end)
                def _():
                    send(z, 1 - x, u, DOWN, last)

            if u >= half:

                @pl.when((t == last) & (z == 1))
                def _(u=u):
                    piece(me, u, CROSS, depth - 2).wait_recv()
                    send(last, 1 - x, u, DOWN, last)

                @pl.when((t == last) & (z == depth - 2))
                def _(u=u):
                    piece(me, u, CROSS, 2).wait_recv()
                    send(0, 1 - x, u, UP, last)

        return carry

    lax.fori_loop(1, depth, step, 0)

    for u in range(count):
        seen = low_end | high_end

        @pl.when(jnp.logical_not(seen))
        def _(u=u):
            piece(me, u, CROSS, 0).wait_recv()

    def remaining(t, carry):
        source = lax.rem(z + t, depth)
        for u in range(count):
            owed = crosses(source, u)
            if u >= half:
                seen = ((z == 1) & (source == last)) | ((z == depth - 2) & (source == 0))
                owed = owed & jnp.logical_not(seen)

            @pl.when(owed)
            def _(u=u):
                piece(me, u, CROSS, t).wait_recv()

        return carry

    lax.fori_loop(1, depth, remaining, 0)
    for u in range(count):
        from_above = (z >= depth // 2) & (z <= depth - 2)
        from_below = (z >= 1) & (z < depth // 2)
        if u >= half:
            from_above = from_above | (z == 0)
            from_below = from_below | (z == last)

        @pl.when(from_above)
        def _(u=u):
            piece(me, u, DOWN, last).wait_recv()

        @pl.when(from_below)
        def _(u=u):
            piece(me, u, UP, last).wait_recv()

    for copy in nrm_copies:
        copy.wait_recv()
    for i in order:
        for copy in sum_copies[i]:
            copy.wait_send()
    for copy in wid_copies + nrm_copies:
        copy.wait_send()

    def sent(t, carry):
        source = lax.rem(z + t, depth)
        for u in range(count):

            @pl.when((z >= 1) & (z + t <= last))
            def _(u=u):
                piece(me, u, DOWN, t).wait_send()

            @pl.when((z <= depth - 2) & (z - t >= 0))
            def _(u=u):
                piece(me, u, UP, t).wait_send()

            @pl.when(crosses(source, u))
            def _(u=u):
                piece(me, u, CROSS, t).wait_send()

        return carry

    lax.fori_loop(0, depth, sent, 0)
    for u in range(count):
        to_above, to_below = low_end, high_end
        if u >= half:
            to_above = to_above | (z == depth - 2)
            to_below = to_below | (z == 1)

        @pl.when(to_above)
        def _(u=u):
            piece(me, u, UP, last).wait_send()

        @pl.when(to_below)
        def _(u=u):
            piece(me, u, DOWN, last).wait_send()


def write_kernel(parts, *refs):
    size = len(refs) - 2
    moved = size // 2
    ins, norm_in, results, norm_out, sems = refs[:moved], refs[moved], refs[moved + 1 : -2], refs[-2], refs[-1]
    copies = []
    for i, (ref, result) in enumerate(zip(ins, results)):
        pieces = parts[i]
        rows = ref.shape[0] // pieces
        for j in range(pieces):
            where = pl.ds(j * rows, rows)
            copy = pltpu.make_async_copy(ref.at[where], result.at[where], sems.at[len(copies)])
            copy.start()
            copies.append(copy)
    norm_out[...] = norm_in[...].astype(jnp.bfloat16)
    for copy in copies:
        copy.wait()


def local(
    n,
    width,
    w_query,
    first_query,
    second_query,
    w_key,
    first_key,
    second_key,
    w_value,
    first_value,
    second_value,
    norm_train,
    norm_step,
):
    groups = ((w_query, first_query, second_query), (w_key, first_key, second_key), (w_value, first_value, second_value))
    rows = w_query.shape[0]
    extents = [each[0].shape[1] for each in groups]
    units = plan_units(rows, extents)
    piece = norm_train.shape[0]
    depth = n // 2
    dma = pltpu.SemaphoreType.DMA
    vmem = pl.BlockSpec(memory_space=pltpu.VMEM)
    hbm = pl.BlockSpec(memory_space=pltpu.HBM)
    shapes = [jax.ShapeDtypeStruct((rows * n, e), jnp.bfloat16) for e in extents]
    shapes += [jax.ShapeDtypeStruct((rows, e), jnp.float32) for e in extents]
    shapes += [jax.ShapeDtypeStruct((1, e), jnp.float32) for e in extents]
    gathered = pl.pallas_call(
        functools.partial(gather_kernel, n, width, units),
        out_shape=shapes + [jax.ShapeDtypeStruct((n, width, 1, piece), jnp.float32)],
        in_specs=[hbm] * 11,
        out_specs=[vmem] * 10,
        scratch_shapes=[pltpu.VMEM((3, rows, e), jnp.float32) for e in extents]
        + [pltpu.VMEM((n, 1, e), jnp.float32) for e in extents]
        + [
            pltpu.VMEM((2, 1, piece), jnp.float32),
            dma((2,)),
            dma((len(units), 3)),
            dma((3, n - 1)),
            dma((3, n - 1)),
            dma((width - 1,)),
            dma((width - 1,)),
            dma((n - 1,)),
            dma((n - 1,)),
            dma((3, depth, len(units))),
            dma((3, depth, len(units))),
        ],
        compiler_params=pltpu.CompilerParams(
            collective_id=0, has_side_effects=True, vmem_limit_bytes=16 * 1024 * 1024
        ),
    )(
        *[pltpu.with_memory_space_constraint(each, pltpu.HBM) for group in groups for each in group],
        pltpu.with_memory_space_constraint(norm_train.reshape(1, -1), pltpu.HBM),
        pltpu.with_memory_space_constraint(norm_step.reshape(1, -1), pltpu.HBM),
    )
    moved, gain = gathered[:-1], gathered[-1].reshape(-1, 128)
    parts = [max(1, each.size * each.dtype.itemsize // (1 << 20)) for each in moved]
    written = pl.pallas_call(
        functools.partial(write_kernel, parts),
        out_shape=shapes + [jax.ShapeDtypeStruct(gain.shape, jnp.bfloat16)],
        in_specs=[vmem] * 10,
        out_specs=[hbm] * 9 + [vmem],
        scratch_shapes=[dma((sum(parts),))],
        compiler_params=pltpu.CompilerParams(vmem_limit_bytes=16 * 1024 * 1024),
    )(*moved, gain)
    serving, whole, column = written[:3], written[3:6], written[6:9]
    return (*serving, *[each.reshape(-1) for each in column], written[9].reshape(-1), *whole)


def solution(mesh):
    split = P("shard", "width")
    both = P(("shard", "width"))
    n, width = mesh.shape["shard"], mesh.shape["width"]
    return jax.shard_map(
        functools.partial(local, n, width),
        mesh=mesh,
        in_specs=(split,) * 9 + (both, both),
        out_specs=(P(None, "width"),) * 3 + (P("width"),) * 3 + (P(),) + (split,) * 3,
        check_vma=False,
    )
```

time: 197 us -> 139 us (0.71)
  Pallas kernels: 176 us -> 139 us
  local copies, waits for them, and re-layouts: 13.1 us -> 0 us
  other arithmetic: 6.96 us -> 0 us
    pallas_call x1 -> x2, Pallas kernels: 176 us -> 139 us  [the longest x1 132 us: local(): pl.pallas_call(functools.partial(gather_kernel, n, width, units), out_sha...]
    unnamed x14 -> x0, local copies, waits for them, and re-layouts: 13.1 us -> none
    sub x2 -> x0, other arithmetic: 5.64 us -> none  [the longest x1 3.45 us: local(): w_query - learn_rate * (hold_rate * first_query + second_query)]
where the time goes in v1:
time: 139 us
  Pallas kernels  139 us (100%)
    pallas_call x1, Pallas kernels, local(): pl.pallas_call(functools.partial(gather_kernel, n, width, units), out_sha...  132 us
    pallas_call x1, Pallas kernels, local(): pl.pallas_call(functools.partial(write_kernel, parts), out_shape=shapes +...  6.27 us

profile of v1, /device:TPU:0, one launch (start us, length us, event | category | flops | bytes accessed | tf_op | source)
XLA Modules:
  0.0 139.3 jit_solution(2085446846126549737)
XLA Ops:
  0.6 132.4 %shard_map.186 = (bf16[4096,1024]{1,0:T(8,128)(2,1)S(1)}, bf16[4096,256]{1,0:T(8,128)(2,1)S(1)}, bf16[4096,256]{1,0:T(8,128)(2,1)S(1)}, f32[512,1024]{1,0:T(8,12...) custom-call(f32[512,1024]{1,0:T(8,128)} %w_q.1, ...), custom_call_target="tpu_custom_call" | custom-call | tf_op jit(solution)/shard_map/pallas_call | solution.py:416
  133.0 6.3 %shard_map.187 = (bf16[4096,1024]{1,0:T(8,128)(2,1)}, bf16[4096,256]{1,0:T(8,128)(2,1)}, bf16[4096,256]{1,0:T(8,128)(2,1)}, f32[512,1024]{1,0:T(8,128)}, f32[512...) custom-call(bf16[4096,1024]{1,0:T(8,128)(2,1)S(1)} %get-tuple-elemen, ...), custom_call_target="tpu_custom_call" | custom-call | tf_op jit(solution)/shard_map/pallas_call | solution.py:446

commit v2 on v1

--- a/solution.py
+++ b/solution.py
@@ -1,4 +1,5 @@
 import functools
+import math
 
 import jax
 import jax.numpy as jnp
@@ -19,9 +20,20 @@
     units = []
     for i in sorted(range(len(extents)), key=lambda i: extents[i]):
         count = max(1, min(extents[i] // least, rows // TILE))
+        if not units:
+            count = max(2, count)
         size = rows // count
         units += [(i, j * size, size) for j in range(count)]
     return units
+
+
+def half_of(units, extents):
+    sizes = [extents[i] * size for i, _, size in units]
+    return min(range(1, len(units)), key=lambda u: abs(2 * sum(sizes[:u]) - sum(sizes)))
+
+
+def loop_rows(size, extent):
+    return math.gcd(size, max(TILE, 16 * 1024 // extent))
 
 
 def gather_kernel(
@@ -57,6 +69,9 @@
     sums_v,
     in_norm,
     norm_sem,
+    in_early,
+    early_send,
+    early_recv,
     load_sem,
     sum_send,
     sum_recv,
@@ -72,11 +87,11 @@
     depth = n // 2
     z, x = lax.div(me, 2), lax.rem(me, 2)
     count = len(units)
-    half = count // 2
     outs, wholes, cols = (out_q, out_k, out_v), (whole_q, whole_k, whole_v), (col_q, col_k, col_v)
     stages, sums = (in_q, in_k, in_v), (sums_q, sums_k, sums_v)
     sources = ((w_q, first_q, second_q), (w_k, first_k, second_k), (w_v, first_v, second_v))
     rows = whole_q.shape[0]
+    half = half_of(units, [each.shape[1] for each in wholes])
     order = list(dict.fromkeys(unit[0] for unit in units))
 
     barrier = pltpu.get_barrier_semaphore()
@@ -96,9 +111,16 @@
             copy = pltpu.make_async_copy(
                 sources[i][j].at[pl.ds(at, size)], stages[i].at[j, pl.ds(at, size)], load_sem.at[u, j]
             )
-            copy.start()
             group.append(copy)
         loads.append(group)
+
+    def load(array_is_first):
+        for (i, _, _), group in zip(units, loads):
+            if (i == order[0]) == array_is_first:
+                for copy in group:
+                    copy.start()
+
+    load(True)
     norm_loads = [
         pltpu.make_async_copy(ref, in_norm.at[j], norm_sem.at[j])
         for j, ref in enumerate((norm_train, norm_step))
@@ -106,32 +128,65 @@
     for copy in norm_loads:
         copy.start()
 
+    targets = (lax.max(z - 1, 0) * 2 + x, lax.min(z + 1, depth - 1) * 2 + x, z * 2 + 1 - x)
+    has = (z >= 1, z <= depth - 2, None)
+    first, early_at, early_size = units[0]
+    parts = early_send.shape[1]
+
+    def early(way, part):
+        size = early_size // parts
+        return pltpu.make_async_remote_copy(
+            src_ref=wholes[first].at[pl.ds(early_at + part * size, size)],
+            dst_ref=in_early.at[way, pl.ds(part * size, size)],
+            send_sem=early_send.at[way, part],
+            recv_sem=early_recv.at[way, part],
+            device_id={"shard": targets[way]},
+            device_id_type=MESH,
+        )
+
+    def both_ways(way, act):
+        if has[way] is None:
+            act()
+        else:
+            pl.when(has[way])(act)
+
+    def send_early(part):
+        for way in range(3):
+            both_ways(way, lambda way=way: early(way, part).start())
+
+    def block_sums(u, total):
+        i, at, size = units[u]
+        stage, whole = stages[i], wholes[i]
+        group = loop_rows(size, whole.shape[1])
+
+        def update(r, total):
+            for j in range(group // 8):
+                here = pl.ds(pl.multiple_of(at + r * group + j * 8, 8), 8)
+                new = stage[0, here] - learn_rate * (hold_rate * stage[1, here] + stage[2, here])
+                whole[here, :] = new
+                total = total + jnp.abs(new)
+            return total
+
+        return lax.fori_loop(0, size // group, update, total)
+
     sum_copies = {}
     wid_copies = []
-    met = False
+    part = 0
     for i in order:
-        stage, whole = stages[i], wholes[i]
-        total = jnp.zeros((8, whole.shape[1]), jnp.float32)
-        for u, (owner, at, size) in enumerate(units):
-            if owner != i:
-                continue
+        mine = [u for u in range(count) if units[u][0] == i]
+        total = jnp.zeros((8, wholes[i].shape[1]), jnp.float32)
+        for u in mine:
             for copy in loads[u]:
                 copy.wait()
-
-            def update(r, total, at=at, stage=stage, whole=whole):
-                for j in range(TILE // 8):
-                    here = pl.ds(pl.multiple_of(at + r * TILE + j * 8, 8), 8)
-                    new = stage[0, here] - learn_rate * (hold_rate * stage[1, here] + stage[2, here])
-                    whole[here, :] = new
-                    total = total + jnp.abs(new)
-                return total
-
-            total = lax.fori_loop(0, size // TILE, update, total)
+        if i == first:
+            load(False)
+        for u in mine:
+            total = block_sums(u, total)
+            if i != first and u == mine[len(mine) // 2] and u != mine[0] and part < parts:
+                send_early(part)
+                part += 1
         sums[i][me] = jnp.sum(total, axis=0, keepdims=True)
-        if not met:
-            for copy in norm_loads:
-                copy.wait()
-            norm_out[me, me_w] = in_norm[0] + in_norm[1]
+        if i == first:
             pl.semaphore_wait(barrier, n - 1 + width - 1)
         sum_copies[i] = []
         for k in range(1, n):
@@ -145,7 +200,13 @@
             )
             copy.start()
             sum_copies[i].append(copy)
-        if not met:
+        if part < parts:
+            send_early(part)
+            part += 1
+        if i == first:
+            for copy in norm_loads:
+                copy.wait()
+            norm_out[me, me_w] = in_norm[0] + in_norm[1]
             for k in range(1, width):
                 copy = pltpu.make_async_remote_copy(
                     src_ref=norm_out.at[me, me_w],
@@ -157,9 +218,8 @@
                 )
                 copy.start()
                 wid_copies.append(copy)
-        met = True
-
-    targets = (lax.max(z - 1, 0) * 2 + x, lax.min(z + 1, depth - 1) * 2 + x, z * 2 + 1 - x)
+    for late in range(part, parts):
+        send_early(late)
 
     def piece(owner, u, way, slot):
         i, at, size = units[u]
@@ -184,6 +244,25 @@
     def send(owner_z, column, u, way, slot):
         piece(owner_z * 2 + column, u, way, slot).start()
 
+    def narrow(source, source_at, owner, u, factor):
+        i, at, size = units[u]
+        out = outs[i]
+        group = loop_rows(size, out.shape[1])
+        scale = jnp.broadcast_to(factor, (group, out.shape[1]))
+
+        def body(r, carry):
+            here = pl.ds(pl.multiple_of(source_at + r * group, TILE), group)
+            there = pl.ds(pl.multiple_of(owner * rows + at + r * group, TILE), group)
+            out[there, :] = (source[here, :] * scale).astype(jnp.bfloat16)
+            return carry
+
+        lax.fori_loop(0, size // group, body, 0)
+
+    def early_arrived(way, owner):
+        for part in range(parts):
+            early(way, part).wait_recv()
+        narrow(in_early.at[way], 0, owner, 0, first_factor)
+
     for i in order:
         for copy in sum_copies[i]:
             copy.wait_recv()
@@ -192,29 +271,19 @@
             total = total + sums[i][k]
         col = total / (rows * n)
         cols[i][...] = col
-        factor = jnp.broadcast_to(1.0 / col, (TILE, col.shape[1]))
-        whole, out = wholes[i], outs[i]
-        for u, (owner, at, size) in enumerate(units):
+        factor = 1.0 / col
+        if i == first:
+            first_factor = factor
+        for u in range(count):
+            owner, at, size = units[u]
             if owner != i:
                 continue
-
-            def narrow(r, carry, at=at, whole=whole, out=out, factor=factor):
-                here = pl.multiple_of(at + r * TILE, TILE)
-                there = pl.multiple_of(me * rows + at + r * TILE, TILE)
-                out[pl.ds(there, TILE), :] = (whole[pl.ds(here, TILE), :] * factor).astype(jnp.bfloat16)
-                return carry
-
-            lax.fori_loop(0, size // TILE, narrow, 0)
-
-            @pl.when(z >= 1)
-            def _(u=u):
-                send(z, x, u, DOWN, 0)
-
-            @pl.when(z <= depth - 2)
-            def _(u=u):
-                send(z, x, u, UP, 0)
-
-            send(z, x, u, CROSS, 0)
+            if u > 0:
+                narrow(wholes[i], at, me, u, factor)
+                for way in range(3):
+                    both_ways(way, lambda u=u, way=way: send(z, x, u, way, 0))
+        if i == first:
+            narrow(wholes[i], early_at, me, 0, factor)
 
     for copy in wid_copies:
         copy.wait_recv()
@@ -234,12 +303,18 @@
     last = depth - 1
     low_end, high_end = z <= depth // 2 - 2, z >= depth // 2 + 1
 
+    def arrived(u, way, t, owner):
+        if u == 0 and isinstance(t, int) and t == 1:
+            early_arrived(way, owner)
+        else:
+            piece(me, u, way, t - 1).wait_recv()
+
     def step(t, carry):
         for u in range(count):
 
             @pl.when(z + t <= last)
             def _(u=u):
-                piece(me, u, DOWN, t - 1).wait_recv()
+                arrived(u, DOWN, t, (z + t) * 2 + x)
 
                 @pl.when(z >= 1)
                 def _():
@@ -251,7 +326,7 @@
 
             @pl.when(z - t >= 0)
             def _(u=u):
-                piece(me, u, UP, t - 1).wait_recv()
+                arrived(u, UP, t, (z - t) * 2 + x)
 
                 @pl.when(z <= depth - 2)
                 def _():
@@ -261,17 +336,22 @@
                 def _():
                     send(z - t, x, u, CROSS, depth - t)
 
-            @pl.when((t == 1) & (low_end | high_end))
-            def _(u=u):
-                piece(me, u, CROSS, 0).wait_recv()
-
-                @pl.when(low_end)
-                def _():
-                    send(z, 1 - x, u, UP, last)
-
-                @pl.when(high_end)
-                def _():
-                    send(z, 1 - x, u, DOWN, last)
+            if isinstance(t, int):
+                if u == 0:
+                    early_arrived(CROSS, z * 2 + 1 - x)
+
+                @pl.when(low_end | high_end)
+                def _(u=u):
+                    if u > 0:
+                        piece(me, u, CROSS, 0).wait_recv()
+
+                    @pl.when(low_end)
+                    def _():
+                        send(z, 1 - x, u, UP, last)
+
+                    @pl.when(high_end)
+                    def _():
+                        send(z, 1 - x, u, DOWN, last)
 
             if u >= half:
 
@@ -287,9 +367,10 @@
 
         return carry
 
-    lax.fori_loop(1, depth, step, 0)
-
-    for u in range(count):
+    step(1, 0)
+    lax.fori_loop(2, depth, step, 0)
+
+    for u in range(1, count):
         seen = low_end | high_end
 
         @pl.when(jnp.logical_not(seen))
@@ -337,22 +418,26 @@
     def sent(t, carry):
         source = lax.rem(z + t, depth)
         for u in range(count):
-
-            @pl.when((z >= 1) & (z + t <= last))
+            begun = (u > 0) | (t > 0)
+
+            @pl.when(begun & (z >= 1) & (z + t <= last))
             def _(u=u):
                 piece(me, u, DOWN, t).wait_send()
 
-            @pl.when((z <= depth - 2) & (z - t >= 0))
+            @pl.when(begun & (z <= depth - 2) & (z - t >= 0))
             def _(u=u):
                 piece(me, u, UP, t).wait_send()
 
-            @pl.when(crosses(source, u))
+            @pl.when(begun & crosses(source, u))
             def _(u=u):
                 piece(me, u, CROSS, t).wait_send()
 
         return carry
 
     lax.fori_loop(0, depth, sent, 0)
+    for part in range(parts):
+        for way in range(3):
+            both_ways(way, lambda way=way, part=part: early(way, part).wait_send())
     for u in range(count):
         to_above, to_below = low_end, high_end
         if u >= half:
@@ -369,11 +454,14 @@
 
 
 def write_kernel(parts, *refs):
-    size = len(refs) - 2
-    moved = size // 2
-    ins, norm_in, results, norm_out, sems = refs[:moved], refs[moved], refs[moved + 1 : -2], refs[-2], refs[-1]
-    copies = []
-    for i, (ref, result) in enumerate(zip(ins, results)):
+    moved = (len(refs) - 4) // 2
+    ins, norm_in, results, norm_out = refs[:moved], refs[moved], refs[moved + 1 : -3], refs[-3]
+    norm, sems = refs[-2:]
+    norm[...] = norm_in[...].astype(jnp.bfloat16)
+    copies = [pltpu.make_async_copy(norm, norm_out, sems.at[0])]
+    copies[0].start()
+    for i in reversed(range(moved)):
+        ref, result = ins[i], results[i]
         pieces = parts[i]
         rows = ref.shape[0] // pieces
         for j in range(pieces):
@@ -381,7 +469,6 @@
             copy = pltpu.make_async_copy(ref.at[where], result.at[where], sems.at[len(copies)])
             copy.start()
             copies.append(copy)
-    norm_out[...] = norm_in[...].astype(jnp.bfloat16)
     for copy in copies:
         copy.wait()
 
@@ -405,6 +492,7 @@
     rows = w_query.shape[0]
     extents = [each[0].shape[1] for each in groups]
     units = plan_units(rows, extents)
+    early_parts = max(1, min(4, units[0][2] // TILE))
     piece = norm_train.shape[0]
     depth = n // 2
     dma = pltpu.SemaphoreType.DMA
@@ -423,6 +511,9 @@
         + [
             pltpu.VMEM((2, 1, piece), jnp.float32),
             dma((2,)),
+            pltpu.VMEM((3, units[0][2], extents[units[0][0]]), jnp.float32),
+            dma((3, early_parts)),
+            dma((3, early_parts)),
             dma((len(units), 3)),
             dma((3, n - 1)),
             dma((3, n - 1)),
@@ -447,8 +538,8 @@
         functools.partial(write_kernel, parts),
         out_shape=shapes + [jax.ShapeDtypeStruct(gain.shape, jnp.bfloat16)],
         in_specs=[vmem] * 10,
-        out_specs=[hbm] * 9 + [vmem],
-        scratch_shapes=[dma((sum(parts),))],
+        out_specs=[hbm] * 10,
+        scratch_shapes=[pltpu.VMEM(gain.shape, jnp.bfloat16), dma((sum(parts) + 1,))],
         compiler_params=pltpu.CompilerParams(vmem_limit_bytes=16 * 1024 * 1024),
     )(*moved, gain)
     serving, whole, column = written[:3], written[3:6], written[6:9]

time: 139 us -> 138 us (level)
  Pallas kernels: 139 us -> 137 us
where the time goes in v2:
time: 138 us
  Pallas kernels  137 us (99%)
    pallas_call x1, Pallas kernels, local(): pl.pallas_call(functools.partial(gather_kernel, n, width, units), out_sha...  132 us
    pallas_call x1, Pallas kernels, local(): pl.pallas_call(functools.partial(write_kernel, parts), out_shape=shapes +...  5.71 us

profile of v2, /device:TPU:0, one launch (start us, length us, event | category | flops | bytes accessed | tf_op | source)
XLA Modules:
  0.0 138.0 jit_solution(10908831127191723569)
XLA Ops:
  0.6 131.6 %shard_map.186 = (bf16[4096,1024]{1,0:T(8,128)(2,1)S(1)}, bf16[4096,256]{1,0:T(8,128)(2,1)S(1)}, bf16[4096,256]{1,0:T(8,128)(2,1)S(1)}, f32[512,1024]{1,0:T(8,12...) custom-call(f32[512,1024]{1,0:T(8,128)} %w_q.1, ...), custom_call_target="tpu_custom_call" | custom-call | tf_op jit(solution)/shard_map/pallas_call | solution.py:504
  132.3 5.7 %shard_map.187 = (bf16[4096,1024]{1,0:T(8,128)(2,1)}, bf16[4096,256]{1,0:T(8,128)(2,1)}, bf16[4096,256]{1,0:T(8,128)(2,1)}, f32[512,1024]{1,0:T(8,128)}, f32[512...) custom-call(bf16[4096,1024]{1,0:T(8,128)(2,1)S(1)} %get-tuple-elemen, ...), custom_call_target="tpu_custom_call" | custom-call | tf_op jit(solution)/shard_map/pallas_call | solution.py:537

commit v3 on v2

v3 whole, which is shorter than its diff:
```python
import functools
import math

import jax
import jax.numpy as jnp
from jax import lax
from jax.experimental import pallas as pl
from jax.experimental.pallas import tpu as pltpu
from jax.sharding import PartitionSpec as P

learn_rate = 0.2
hold_rate = 0.8
MESH = pl.DeviceIdType.MESH
TILE = 16
DOWN, UP, CROSS = 0, 1, 2


def plan_units(rows, extents):
    least = min(extents)
    units = []
    for i in sorted(range(len(extents)), key=lambda i: extents[i]):
        count = max(1, min(extents[i] // least, rows // TILE))
        size = rows // count
        units += [(i, j * size, size) for j in range(count)]
    return units


def half_of(units, extents):
    sizes = [extents[i] * size for i, _, size in units]
    return min(range(1, len(units)), key=lambda u: abs(2 * sum(sizes[:u]) - sum(sizes)))


def loop_rows(size, extent):
    return math.gcd(size, max(TILE, 16 * 1024 // extent))


def gather_kernel(
    n,
    width,
    units,
    w_q,
    first_q,
    second_q,
    w_k,
    first_k,
    second_k,
    w_v,
    first_v,
    second_v,
    norm_train,
    norm_step,
    out_q,
    out_k,
    out_v,
    whole_q,
    whole_k,
    whole_v,
    col_q,
    col_k,
    col_v,
    norm_out,
    in_q,
    in_k,
    in_v,
    sums_q,
    sums_k,
    sums_v,
    in_norm,
    norm_sem,
    load_sem,
    sum_send,
    sum_recv,
    wid_send,
    wid_recv,
    nrm_send,
    nrm_recv,
    link_send,
    link_recv,
):
    me = lax.axis_index("shard")
    me_w = lax.axis_index("width")
    depth = n // 2
    z, x = lax.div(me, 2), lax.rem(me, 2)
    count = len(units)
    outs, wholes, cols = (out_q, out_k, out_v), (whole_q, whole_k, whole_v), (col_q, col_k, col_v)
    stages, sums = (in_q, in_k, in_v), (sums_q, sums_k, sums_v)
    sources = ((w_q, first_q, second_q), (w_k, first_k, second_k), (w_v, first_v, second_v))
    rows = whole_q.shape[0]
    half = half_of(units, [each.shape[1] for each in wholes])
    order = list(dict.fromkeys(unit[0] for unit in units))

    barrier = pltpu.get_barrier_semaphore()
    for k in range(1, n):
        pl.semaphore_signal(
            barrier, inc=1, device_id={"shard": lax.rem(me + k, n)}, device_id_type=MESH
        )
    for k in range(1, width):
        pl.semaphore_signal(
            barrier, inc=1, device_id={"width": lax.rem(me_w + k, width)}, device_id_type=MESH
        )

    loads = []
    for u, (i, at, size) in enumerate(units):
        group = []
        for j in range(3):
            copy = pltpu.make_async_copy(
                sources[i][j].at[pl.ds(at, size)], stages[i].at[j, pl.ds(at, size)], load_sem.at[u]
            )
            group.append(copy)
        loads.append(group)

    def load(array_is_first):
        for (i, _, _), group in zip(units, loads):
            if (i == order[0]) == array_is_first:
                for copy in group:
                    copy.start()

    load(True)
    norm_loads = [
        pltpu.make_async_copy(ref, in_norm.at[j], norm_sem)
        for j, ref in enumerate((norm_train, norm_step))
    ]
    for copy in norm_loads:
        copy.start()

    targets = (lax.max(z - 1, 0) * 2 + x, lax.min(z + 1, depth - 1) * 2 + x, z * 2 + 1 - x)
    has = (z >= 1, z <= depth - 2, None)
    first = units[0][0]

    def both_ways(way, act):
        if has[way] is None:
            act()
        else:
            pl.when(has[way])(act)

    def block_sums(u, total):
        i, at, size = units[u]
        stage, whole = stages[i], wholes[i]
        group = loop_rows(size, whole.shape[1])

        def update(r, total):
            for j in range(group // 8):
                here = pl.ds(pl.multiple_of(at + r * group + j * 8, 8), 8)
                new = stage[0, here] - learn_rate * (hold_rate * stage[1, here] + stage[2, here])
                whole[here, :] = new
                total = total + jnp.abs(new)
            return total

        return lax.fori_loop(0, size // group, update, total)

    for i in order:
        mine = [u for u in range(count) if units[u][0] == i]
        total = jnp.zeros((8, wholes[i].shape[1]), jnp.float32)
        for u in mine:
            _, at, size = units[u]
            whole_load = stages[i].at[:, pl.ds(at, size)]
            pltpu.make_async_copy(whole_load, whole_load, load_sem.at[u]).wait()
            if u == 0:
                load(False)
            total = block_sums(u, total)
        sums[i][me] = jnp.sum(total, axis=0, keepdims=True)
        if i == first:
            pl.semaphore_wait(barrier, n - 1 + width - 1)
        for k in range(1, n):
            copy = pltpu.make_async_remote_copy(
                src_ref=sums[i].at[me],
                dst_ref=sums[i].at[me],
                send_sem=sum_send.at[i],
                recv_sem=sum_recv.at[i],
                device_id={"shard": lax.rem(me + k, n)},
                device_id_type=MESH,
            )
            copy.start()
        if i == first:
            pltpu.make_async_copy(in_norm, in_norm, norm_sem).wait()
            norm_out[me, me_w] = in_norm[0] + in_norm[1]
            for k in range(1, width):
                copy = pltpu.make_async_remote_copy(
                    src_ref=norm_out.at[me, me_w],
                    dst_ref=norm_out.at[me, me_w],
                    send_sem=wid_send,
                    recv_sem=wid_recv,
                    device_id={"width": lax.rem(me_w + k, width)},
                    device_id_type=MESH,
                )
                copy.start()

    def joint(ref, send_sem, recv_sem):
        return pltpu.make_async_remote_copy(
            src_ref=ref,
            dst_ref=ref,
            send_sem=send_sem,
            recv_sem=recv_sem,
            device_id={"shard": targets[CROSS]},
            device_id_type=MESH,
        )

    halves = (range(half), range(half, count))
    widest = max(range(3), key=lambda i: outs[i].shape[1])

    def bundle(g, way, slot):
        words = sum(units[u][2] * outs[units[u][0]].shape[1] for u in halves[g])
        ref = outs[widest].at[pl.ds(0, words // outs[widest].shape[1])]
        return joint(ref, link_send.at[way, slot, g], link_recv.at[way, slot, g])

    def send_unit(owner_z, column, u, way, slot):
        i, at, size = units[u]
        owner = owner_z * 2 + column
        where = pl.ds(pl.multiple_of(owner * rows + at, TILE), size)
        g = int(u >= half)
        pltpu.make_async_remote_copy(
            src_ref=outs[i].at[where],
            dst_ref=outs[i].at[where],
            send_sem=link_send.at[way, slot, g],
            recv_sem=link_recv.at[way, slot, g],
            device_id={"shard": targets[way]},
            device_id_type=MESH,
        ).start()

    def send(owner_z, column, g, way, slot):
        for u in halves[g]:
            send_unit(owner_z, column, u, way, slot)

    def crosses(source, g):
        low = (z >= 1) & (z < depth // 2) & (source == z - 1)
        high = (z >= depth // 2) & (z <= depth - 2) & (source == z + 1)
        no = low | high
        if g == 1:
            no = no | ((z == 0) & (source == depth - 1)) | ((z == depth - 1) & (source == 0))
        return jnp.logical_not(no)

    def narrow(source, source_at, owner, u, factor):
        i, at, size = units[u]
        out = outs[i]
        group = loop_rows(size, out.shape[1])
        scale = jnp.broadcast_to(factor, (group, out.shape[1]))

        def body(r, carry):
            here = pl.ds(pl.multiple_of(source_at + r * group, TILE), group)
            there = pl.ds(pl.multiple_of(owner * rows + at + r * group, TILE), group)
            out[there, :] = (source[here, :] * scale).astype(jnp.bfloat16)
            return carry

        lax.fori_loop(0, size // group, body, 0)

    for i in order:
        joint(sums[i].at[pl.ds(0, n - 1)], sum_send.at[i], sum_recv.at[i]).wait_recv()
        total = sums[i][0]
        for k in range(1, n):
            total = total + sums[i][k]
        col = total / (rows * n)
        cols[i][...] = col
        factor = 1.0 / col
        for u in range(count):
            owner, at, size = units[u]
            if owner != i:
                continue
            narrow(wholes[i], at, me, u, factor)
            for way in range(3):
                both_ways(way, lambda u=u, way=way: send_unit(z, x, u, way, 0))

    joint(norm_out.at[0, pl.ds(0, width - 1)], wid_send, wid_recv).wait_recv()
    for k in range(1, n):
        copy = pltpu.make_async_remote_copy(
            src_ref=norm_out.at[me],
            dst_ref=norm_out.at[me],
            send_sem=nrm_send,
            recv_sem=nrm_recv,
            device_id={"shard": lax.rem(me + k, n)},
            device_id_type=MESH,
        )
        copy.start()

    last = depth - 1
    low_end, high_end = z <= depth // 2 - 2, z >= depth // 2 + 1

    def step(t, carry):
        for g in range(2):

            @pl.when(z + t <= last)
            def _(g=g):
                bundle(g, DOWN, t - 1).wait_recv()

                @pl.when(z >= 1)
                def _():
                    send(z + t, x, g, DOWN, t)

                swap = (z == 1) & (z + t == last)
                across(z + t, g, t, swap)

            @pl.when(z - t >= 0)
            def _(g=g):
                bundle(g, UP, t - 1).wait_recv()

                @pl.when(z <= depth - 2)
                def _():
                    send(z - t, x, g, UP, t)

                swap = (z == depth - 2) & (z == t)
                across(z - t, g, depth - t, swap)

            @pl.when((t == 1) & (low_end | high_end))
            def _(g=g):
                bundle(g, CROSS, 0).wait_recv()

                @pl.when(low_end)
                def _():
                    send(z, 1 - x, g, UP, last)

                @pl.when(high_end)
                def _():
                    send(z, 1 - x, g, DOWN, last)

        @pl.when((t == last) & (z == 1))
        def _():
            bundle(1, CROSS, depth - 2).wait_recv()
            send(last, 1 - x, 1, DOWN, last)

        @pl.when((t == last) & (z == depth - 2))
        def _():
            bundle(1, CROSS, 2).wait_recv()
            send(0, 1 - x, 1, UP, last)

        return carry

    def across(source, g, slot, swap):
        if g == 0:

            @pl.when(crosses(source, 0) & jnp.logical_not(swap))
            def _():
                send(source, x, 0, CROSS, slot)
        else:

            @pl.when(crosses(source, 1))
            def _():
                send(source, x, 1, CROSS, slot)

            @pl.when(crosses(source, 0) & swap)
            def _():
                send(source, x, 0, CROSS, slot)

    lax.fori_loop(1, depth, step, 0)

    joint(norm_out.at[0, pl.ds(0, width - 1)], wid_send, wid_recv).wait_send()
    for i in order:
        joint(sums[i].at[pl.ds(0, n - 1)], sum_send.at[i], sum_recv.at[i]).wait_send()
    joint(norm_out.at[pl.ds(0, n - 1)], nrm_send, nrm_recv).wait()

    def owed(source, g):
        seen = (source == z) & (low_end | high_end)
        if g == 1:
            seen = seen | ((z == 1) & (source == last)) | ((z == depth - 2) & (source == 0))
        return crosses(source, g) & jnp.logical_not(seen)

    def rest(t, carry):
        above, below = z + t, z - t
        for g in range(2):

            @pl.when((above <= last) & (z >= 1))
            def _(g=g):
                bundle(g, DOWN, t).wait_send()

            @pl.when((below >= 0) & (z <= depth - 2))
            def _(g=g):
                bundle(g, UP, t).wait_send()

            for source, slot, there in (
                (above, t, above <= last),
                (below, depth - t, (t > 0) & (below >= 0)),
            ):

                @pl.when(there & crosses(source, g))
                def _(g=g, slot=slot):
                    bundle(g, CROSS, slot).wait_send()

                @pl.when(there & owed(source, g))
                def _(g=g, slot=slot):
                    bundle(g, CROSS, slot).wait_recv()

        return carry

    lax.fori_loop(0, depth, rest, 0)
    for g in range(2):
        to_above, to_below = low_end, high_end
        from_above = (z >= depth // 2) & (z <= depth - 2)
        from_below = (z >= 1) & (z < depth // 2)
        if g == 1:
            to_above, to_below = to_above | (z == depth - 2), to_below | (z == 1)
            from_above, from_below = from_above | (z == 0), from_below | (z == last)

        @pl.when(to_above)
        def _(g=g):
            bundle(g, UP, last).wait_send()

        @pl.when(to_below)
        def _(g=g):
            bundle(g, DOWN, last).wait_send()

        @pl.when(from_above)
        def _(g=g):
            bundle(g, DOWN, last).wait_recv()

        @pl.when(from_below)
        def _(g=g):
            bundle(g, UP, last).wait_recv()


def write_kernel(*refs):
    moved = (len(refs) - 4) // 2
    ins, norm_in, results, norm_out = refs[:moved], refs[moved], refs[moved + 1 : -3], refs[-3]
    norm, sems = refs[-2:]
    copies = [pltpu.make_async_copy(ins[i], results[i], sems.at[i]) for i in range(moved)]
    for copy in copies:
        copy.start()
    norm[...] = norm_in[...].astype(jnp.bfloat16)
    copies.append(pltpu.make_async_copy(norm, norm_out, sems.at[moved]))
    copies[-1].start()
    for copy in copies:
        copy.wait()


def local(
    n,
    width,
    w_query,
    first_query,
    second_query,
    w_key,
    first_key,
    second_key,
    w_value,
    first_value,
    second_value,
    norm_train,
    norm_step,
):
    groups = ((w_query, first_query, second_query), (w_key, first_key, second_key), (w_value, first_value, second_value))
    rows = w_query.shape[0]
    extents = [each[0].shape[1] for each in groups]
    units = plan_units(rows, extents)
    piece = norm_train.shape[0]
    depth = n // 2
    dma = pltpu.SemaphoreType.DMA
    vmem = pl.BlockSpec(memory_space=pltpu.VMEM)
    hbm = pl.BlockSpec(memory_space=pltpu.HBM)
    shapes = [jax.ShapeDtypeStruct((rows * n, e), jnp.bfloat16) for e in extents]
    shapes += [jax.ShapeDtypeStruct((rows, e), jnp.float32) for e in extents]
    shapes += [jax.ShapeDtypeStruct((1, e), jnp.float32) for e in extents]
    gathered = pl.pallas_call(
        functools.partial(gather_kernel, n, width, units),
        out_shape=shapes + [jax.ShapeDtypeStruct((n, width, 1, piece), jnp.float32)],
        in_specs=[hbm] * 11,
        out_specs=[vmem] * 10,
        scratch_shapes=[pltpu.VMEM((3, rows, e), jnp.float32) for e in extents]
        + [pltpu.VMEM((n, 1, e), jnp.float32) for e in extents]
        + [
            pltpu.VMEM((2, 1, piece), jnp.float32),
            dma(()),
            dma((len(units),)),
            dma((3,)),
            dma((3,)),
            dma(()),
            dma(()),
            dma(()),
            dma(()),
            dma((3, depth, 2)),
            dma((3, depth, 2)),
        ],
        compiler_params=pltpu.CompilerParams(
            collective_id=0, has_side_effects=True, vmem_limit_bytes=16 * 1024 * 1024
        ),
    )(
        *[pltpu.with_memory_space_constraint(each, pltpu.HBM) for group in groups for each in group],
        pltpu.with_memory_space_constraint(norm_train.reshape(1, -1), pltpu.HBM),
        pltpu.with_memory_space_constraint(norm_step.reshape(1, -1), pltpu.HBM),
    )
    moved, gain = gathered[:-1], gathered[-1].reshape(-1, 128)
    written = pl.pallas_call(
        write_kernel,
        out_shape=shapes + [jax.ShapeDtypeStruct(gain.shape, jnp.bfloat16)],
        in_specs=[vmem] * 10,
        out_specs=[hbm] * 10,
        scratch_shapes=[pltpu.VMEM(gain.shape, jnp.bfloat16), dma((len(moved) + 1,))],
        compiler_params=pltpu.CompilerParams(vmem_limit_bytes=16 * 1024 * 1024),
    )(*moved, gain)
    serving, whole, column = written[:3], written[3:6], written[6:9]
    return (*serving, *[each.reshape(-1) for each in column], written[9].reshape(-1), *whole)


def solution(mesh):
    split = P("shard", "width")
    both = P(("shard", "width"))
    n, width = mesh.shape["shard"], mesh.shape["width"]
    return jax.shard_map(
        functools.partial(local, n, width),
        mesh=mesh,
        in_specs=(split,) * 9 + (both, both),
        out_specs=(P(None, "width"),) * 3 + (P("width"),) * 3 + (P(),) + (split,) * 3,
        check_vma=False,
    )
```

time: 138 us -> 136 us (0.986)
  Pallas kernels: 137 us -> 135 us
    pallas_call x1, Pallas kernels: 132 us -> 129 us  [local(): pl.pallas_call(functools.partial(gather_kernel, n, width, units), out_sha...]
where the time goes in v3:
time: 136 us; the launch traced here: 135 us
  Pallas kernels  135 us (99%)
    pallas_call x1, Pallas kernels, local(): pl.pallas_call(functools.partial(gather_kernel, n, width, units), out_sha...  129 us
    pallas_call x1, Pallas kernels, local(): pl.pallas_call(write_kernel, out_shape=shapes + [jax.ShapeDtypeStruct(gai...  5.71 us

profile of v3, /device:TPU:0, one launch (start us, length us, event | category | flops | bytes accessed | tf_op | source)
XLA Modules:
  0.0 135.4 jit_solution(14187662006515756983)
XLA Ops:
  0.6 129.0 %shard_map.186 = (bf16[4096,1024]{1,0:T(8,128)(2,1)S(1)}, bf16[4096,256]{1,0:T(8,128)(2,1)S(1)}, bf16[4096,256]{1,0:T(8,128)(2,1)S(1)}, f32[512,1024]{1,0:T(8,12...) custom-call(f32[512,1024]{1,0:T(8,128)} %w_q.1, ...), custom_call_target="tpu_custom_call" | custom-call | tf_op jit(solution)/shard_map/pallas_call | solution.py:449
  129.7 5.7 %shard_map.187 = (bf16[4096,1024]{1,0:T(8,128)(2,1)}, bf16[4096,256]{1,0:T(8,128)(2,1)}, bf16[4096,256]{1,0:T(8,128)(2,1)}, f32[512,1024]{1,0:T(8,128)}, f32[512...) custom-call(bf16[4096,1024]{1,0:T(8,128)(2,1)S(1)} %get-tuple-elemen, ...), custom_call_target="tpu_custom_call" | custom-call | tf_op jit(solution)/shard_map/pallas_call | solution.py:478

commit v4 on v3

v4 whole, which is shorter than its diff:
```python
import functools
import math

import jax
import jax.numpy as jnp
from jax import lax
from jax.experimental import pallas as pl
from jax.experimental.pallas import tpu as pltpu
from jax.sharding import PartitionSpec as P

learn_rate = 0.2
hold_rate = 0.8
MESH = pl.DeviceIdType.MESH
TILE = 16
DOWN, UP, CROSS = 0, 1, 2


def plan_units(rows, extents):
    wide = extents.index(max(extents))
    units = [(i, 0, rows) for i in range(len(extents)) if i != wide]
    count = 8 if rows % (8 * TILE) == 0 else 4
    return units + [(wide, j * (rows // count), rows // count) for j in range(count)]


def plan_stages(units, extents):
    wide = units[-1][0]
    narrow = [u for u, unit in enumerate(units) if unit[0] != wide]
    rest = [u for u, unit in enumerate(units) if unit[0] == wide]
    count = len(rest)
    cuts = (count // 2, 3 * count // 4) if count >= 8 else (count // 2,)

    def split(chosen):
        sizes = [extents[units[u][0]] * units[u][2] for u in chosen]
        at = min(range(1, len(chosen)), key=lambda k: abs(2 * sum(sizes[:k]) - sum(sizes)))
        return chosen[:at], chosen[at:]

    return [(split(narrow + rest[:cut]), split(rest[cut:])) for cut in cuts]


def loop_rows(size, extent):
    return math.gcd(size, max(TILE, 16 * 1024 // extent))


class Ladder:
    def __init__(self, n, units, halves, place, spare, link_send, link_recv):
        self.depth, self.units, self.halves, self.place, self.spare = n // 2, units, halves, place, spare
        self.link_send, self.link_recv = link_send, link_recv
        me = lax.axis_index("shard")
        self.z, self.x = z, x = lax.div(me, 2), lax.rem(me, 2)
        self.last = last = self.depth - 1
        self.targets = (lax.max(z - 1, 0) * 2 + x, lax.min(z + 1, last) * 2 + x, z * 2 + 1 - x)
        self.low_end, self.high_end = z <= self.depth // 2 - 2, z >= self.depth // 2 + 1

    def joint(self, ref, send_sem, recv_sem):
        return pltpu.make_async_remote_copy(
            src_ref=ref,
            dst_ref=ref,
            send_sem=send_sem,
            recv_sem=recv_sem,
            device_id={"shard": self.targets[CROSS]},
            device_id_type=MESH,
        )

    def bundle(self, g, way, slot):
        words = sum(self.units[u][2] * self.place(u, 0)[0].shape[1] for u in self.halves[g])
        ref = self.spare.at[pl.ds(0, words // self.spare.shape[1])]
        return self.joint(ref, self.link_send.at[way, slot, g], self.link_recv.at[way, slot, g])

    def send_unit(self, owner_z, column, u, way, slot):
        ref, at = self.place(u, owner_z * 2 + column)
        where = pl.ds(pl.multiple_of(at, TILE), self.units[u][2])
        g = int(u in self.halves[1])
        pltpu.make_async_remote_copy(
            src_ref=ref.at[where],
            dst_ref=ref.at[where],
            send_sem=self.link_send.at[way, slot, g],
            recv_sem=self.link_recv.at[way, slot, g],
            device_id={"shard": self.targets[way]},
            device_id_type=MESH,
        ).start()

    def send(self, owner_z, column, g, way, slot):
        for u in self.halves[g]:
            self.send_unit(owner_z, column, u, way, slot)

    def send_own(self, u):
        z, x = self.z, self.x

        @pl.when(z >= 1)
        def _():
            self.send_unit(z, x, u, DOWN, 0)

        @pl.when(z <= self.last - 1)
        def _():
            self.send_unit(z, x, u, UP, 0)

        self.send_unit(z, x, u, CROSS, 0)

    def crosses(self, source, g):
        z, depth, last = self.z, self.depth, self.last
        low = (z >= 1) & (z < depth // 2) & (source == z - 1)
        high = (z >= depth // 2) & (z <= depth - 2) & (source == z + 1)
        no = low | high
        if g == 1:
            no = no | ((z == 0) & (source == last)) | ((z == last) & (source == 0))
        return jnp.logical_not(no)

    def across(self, source, g, slot, swap):
        if g == 0:

            @pl.when(self.crosses(source, 0) & jnp.logical_not(swap))
            def _():
                self.send(source, self.x, 0, CROSS, slot)
        else:

            @pl.when(self.crosses(source, 1))
            def _():
                self.send(source, self.x, 1, CROSS, slot)

            @pl.when(self.crosses(source, 0) & swap)
            def _():
                self.send(source, self.x, 0, CROSS, slot)

    def step(self, t, carry):
        z, x, depth, last = self.z, self.x, self.depth, self.last
        for g in range(2):

            @pl.when(z + t <= last)
            def _(g=g):
                self.bundle(g, DOWN, t - 1).wait_recv()

                @pl.when(z >= 1)
                def _():
                    self.send(z + t, x, g, DOWN, t)

                self.across(z + t, g, t, (z == 1) & (z + t == last))

            @pl.when(z - t >= 0)
            def _(g=g):
                self.bundle(g, UP, t - 1).wait_recv()

                @pl.when(z <= depth - 2)
                def _():
                    self.send(z - t, x, g, UP, t)

                self.across(z - t, g, depth - t, (z == depth - 2) & (z == t))

            @pl.when((t == 1) & (self.low_end | self.high_end))
            def _(g=g):
                self.bundle(g, CROSS, 0).wait_recv()

                @pl.when(self.low_end)
                def _():
                    self.send(z, 1 - x, g, UP, last)

                @pl.when(self.high_end)
                def _():
                    self.send(z, 1 - x, g, DOWN, last)

        @pl.when((t == last) & (z == 1))
        def _():
            self.bundle(1, CROSS, depth - 2).wait_recv()
            self.send(last, 1 - x, 1, DOWN, last)

        @pl.when((t == last) & (z == depth - 2))
        def _():
            self.bundle(1, CROSS, 2).wait_recv()
            self.send(0, 1 - x, 1, UP, last)

        return carry

    def run(self):
        lax.fori_loop(1, self.depth, self.step, 0)

    def finish(self):
        z, depth, last = self.z, self.depth, self.last

        def owed(source, g):
            seen = (source == z) & (self.low_end | self.high_end)
            if g == 1:
                seen = seen | ((z == 1) & (source == last)) | ((z == depth - 2) & (source == 0))
            return self.crosses(source, g) & jnp.logical_not(seen)

        def rest(t, carry):
            above, below = z + t, z - t
            for g in range(2):

                @pl.when((above <= last) & (z >= 1))
                def _(g=g):
                    self.bundle(g, DOWN, t).wait_send()

                @pl.when((below >= 0) & (z <= depth - 2))
                def _(g=g):
                    self.bundle(g, UP, t).wait_send()

                for source, slot, there in (
                    (above, t, above <= last),
                    (below, depth - t, (t > 0) & (below >= 0)),
                ):

                    @pl.when(there & self.crosses(source, g))
                    def _(g=g, slot=slot):
                        self.bundle(g, CROSS, slot).wait_send()

                    @pl.when(there & owed(source, g))
                    def _(g=g, slot=slot):
                        self.bundle(g, CROSS, slot).wait_recv()

            return carry

        lax.fori_loop(0, depth, rest, 0)
        for g in range(2):
            to_above, to_below = self.low_end, self.high_end
            from_above = (z >= depth // 2) & (z <= depth - 2)
            from_below = (z >= 1) & (z < depth // 2)
            if g == 1:
                to_above, to_below = to_above | (z == depth - 2), to_below | (z == 1)
                from_above, from_below = from_above | (z == 0), from_below | (z == last)

            @pl.when(to_above)
            def _(g=g):
                self.bundle(g, UP, last).wait_send()

            @pl.when(to_below)
            def _(g=g):
                self.bundle(g, DOWN, last).wait_send()

            @pl.when(from_above)
            def _(g=g):
                self.bundle(g, DOWN, last).wait_recv()

            @pl.when(from_below)
            def _(g=g):
                self.bundle(g, UP, last).wait_recv()


def by_core(count, body):
    if count == 1:
        body(0)
        return
    core = lax.rem(lax.axis_index("width"), 2)
    for c in range(2):
        pl.when(core == c)(functools.partial(body, c))


def scaled(source, source_at, target, target_at, size, factor):
    extent = target.shape[1]
    group = loop_rows(size, extent)
    scale = jnp.broadcast_to(factor, (group, extent))

    def body(r, carry):
        here = pl.ds(pl.multiple_of(source_at + r * group, TILE), group)
        there = pl.ds(pl.multiple_of(target_at + r * group, TILE), group)
        target[there, :] = (source[here, :] * scale).astype(jnp.bfloat16)
        return carry

    lax.fori_loop(0, size // group, body, 0)


def gather_kernel(
    n,
    width,
    units,
    stages,
    w_q,
    first_q,
    second_q,
    w_k,
    first_k,
    second_k,
    w_v,
    first_v,
    second_v,
    norm_train,
    norm_step,
    low,
    out_k,
    out_v,
    mid,
    whole_q,
    whole_k,
    whole_v,
    col_q,
    col_k,
    col_v,
    norm_out,
    in_q,
    in_k,
    in_v,
    sums_q,
    sums_k,
    sums_v,
    in_norm,
    norm_sem,
    load_sem,
    sum_send,
    sum_recv,
    wid_send,
    wid_recv,
    nrm_send,
    nrm_recv,
    link_send,
    link_recv,
):
    me = lax.axis_index("shard")
    me_w = lax.axis_index("width")
    wholes, cols = (whole_q, whole_k, whole_v), (col_q, col_k, col_v)
    staged, sums = (in_q, in_k, in_v), (sums_q, sums_k, sums_v)
    sources = ((w_q, first_q, second_q), (w_k, first_k, second_k), (w_v, first_v, second_v))
    rows = whole_q.shape[0]
    count = len(units)
    order = list(dict.fromkeys(unit[0] for unit in units))

    barrier = pltpu.get_barrier_semaphore()
    for k in range(1, n):
        pl.semaphore_signal(
            barrier, inc=1, device_id={"shard": lax.rem(me + k, n)}, device_id_type=MESH
        )
    for k in range(1, width):
        pl.semaphore_signal(
            barrier, inc=1, device_id={"width": lax.rem(me_w + k, width)}, device_id_type=MESH
        )

    loads = []
    for u, (i, at, size) in enumerate(units):
        group = []
        for j in range(3):
            copy = pltpu.make_async_copy(
                sources[i][j].at[pl.ds(at, size)], staged[i].at[j, pl.ds(at, size)], load_sem.at[u]
            )
            group.append(copy)
        loads.append(group)

    def load(array_is_first):
        for (i, _, _), group in zip(units, loads):
            if (i == order[0]) == array_is_first:
                for copy in group:
                    copy.start()

    load(True)
    norm_loads = [
        pltpu.make_async_copy(ref, in_norm.at[j], norm_sem)
        for j, ref in enumerate((norm_train, norm_step))
    ]
    for copy in norm_loads:
        copy.start()

    first = units[0][0]

    def block_sums(u, total):
        i, at, size = units[u]
        stage, whole = staged[i], wholes[i]
        group = loop_rows(size, whole.shape[1])

        def update(r, total):
            for j in range(group // 8):
                here = pl.ds(pl.multiple_of(at + r * group + j * 8, 8), 8)
                new = stage[0, here] - learn_rate * (hold_rate * stage[1, here] + stage[2, here])
                whole[here, :] = new
                total = total + jnp.abs(new)
            return total

        return lax.fori_loop(0, size // group, update, total)

    for i in order:
        mine = [u for u in range(count) if units[u][0] == i]
        total = jnp.zeros((8, wholes[i].shape[1]), jnp.float32)
        for u in mine:
            _, at, size = units[u]
            whole_load = staged[i].at[:, pl.ds(at, size)]
            pltpu.make_async_copy(whole_load, whole_load, load_sem.at[u]).wait()
            if u == 0:
                load(False)
            total = block_sums(u, total)
        sums[i][me] = jnp.sum(total, axis=0, keepdims=True)
        if i == first:
            pl.semaphore_wait(barrier, n - 1 + width - 1)
        for k in range(1, n):
            copy = pltpu.make_async_remote_copy(
                src_ref=sums[i].at[me],
                dst_ref=sums[i].at[me],
                send_sem=sum_send.at[i],
                recv_sem=sum_recv.at[i],
                device_id={"shard": lax.rem(me + k, n)},
                device_id_type=MESH,
            )
            copy.start()
        if i == first:
            pltpu.make_async_copy(in_norm, in_norm, norm_sem).wait()
            norm_out[me, me_w] = in_norm[0] + in_norm[1]
            for k in range(1, width):
                copy = pltpu.make_async_remote_copy(
                    src_ref=norm_out.at[me, me_w],
                    dst_ref=norm_out.at[me, me_w],
                    send_sem=wid_send,
                    recv_sem=wid_recv,
                    device_id={"width": lax.rem(me_w + k, width)},
                    device_id_type=MESH,
                )
                copy.start()

    def place(u, owner):
        i, at, _ = units[u]
        if i == 1 or i == 2:
            return (out_k, out_v)[i - 1], owner * rows + at
        if at < rows // 2:
            return low, owner * (rows // 2) + at
        return mid, owner * (rows // 4) + at - rows // 2

    def body(c):
        halves = stages[c][0]
        mine = halves[0] + halves[1]
        ladder = Ladder(n, units, halves, place, low, link_send, link_recv)
        for i in order:
            ladder.joint(sums[i].at[pl.ds(0, n - 1)], sum_send.at[i], sum_recv.at[i]).wait_recv()
            total = sums[i][0]
            for k in range(1, n):
                total = total + sums[i][k]
            col = total / (rows * n)
            cols[i][...] = col
            factor = 1.0 / col
            for u in mine:
                owner, at, size = units[u]
                if owner == i:
                    ref, there = place(u, me)
                    scaled(wholes[i], at, ref, there, size, factor)
                    ladder.send_own(u)
        ladder.joint(norm_out.at[0, pl.ds(0, width - 1)], wid_send, wid_recv).wait_recv()
        for k in range(1, n):
            pltpu.make_async_remote_copy(
                src_ref=norm_out.at[me],
                dst_ref=norm_out.at[me],
                send_sem=nrm_send,
                recv_sem=nrm_recv,
                device_id={"shard": lax.rem(me + k, n)},
                device_id_type=MESH,
            ).start()
        ladder.run()
        ladder.joint(norm_out.at[0, pl.ds(0, width - 1)], wid_send, wid_recv).wait_send()
        for i in order:
            ladder.joint(sums[i].at[pl.ds(0, n - 1)], sum_send.at[i], sum_recv.at[i]).wait_send()
        ladder.joint(norm_out.at[pl.ds(0, n - 1)], nrm_send, nrm_recv).wait()
        ladder.finish()

    by_core(len(stages), body)


def write_first_kernel(
    n,
    kinds,
    low,
    out_k,
    out_v,
    mid,
    whole_q,
    whole_k,
    whole_v,
    col_q,
    col_k,
    col_v,
    norm_in,
    to_q,
    to_k,
    to_v,
    to_whole_q,
    to_whole_k,
    to_whole_v,
    to_col_q,
    to_col_k,
    to_col_v,
    to_norm,
    own,
    norm,
    sems,
):
    rows = whole_q.shape[0]
    pairs = (
        (out_k, to_k),
        (out_v, to_v),
        (whole_q, to_whole_q),
        (whole_k, to_whole_k),
        (whole_v, to_whole_v),
        (col_q, to_col_q),
        (col_k, to_col_k),
        (col_v, to_col_v),
    )
    for j, (ref, result) in enumerate(pairs):
        pltpu.make_async_copy(ref, result, sems.at[j]).start()
    spread(n, rows, low, to_q, 0, sems.at[8])

    def more(c):
        if c == 1:
            spread(n, rows, mid, to_q, rows // 2, sems.at[9])

    by_core(kinds, more)
    norm[...] = norm_in[...].astype(jnp.bfloat16)
    pltpu.make_async_copy(norm, to_norm, sems.at[10]).start()
    scaled(whole_q, rows // 2, own, 0, rows // 2, 1.0 / col_q[...])

    def end(c):
        if c == 1:
            pltpu.make_async_copy(mid, mid, sems.at[9]).wait()

    for j, (ref, result) in enumerate(pairs):
        pltpu.make_async_copy(ref, result, sems.at[j]).wait()
    pltpu.make_async_copy(low, low, sems.at[8]).wait()
    by_core(kinds, end)
    pltpu.make_async_copy(norm, to_norm, sems.at[10]).wait()


def spread(n, rows, ref, result, at, sem):
    size = ref.shape[0] // n

    def body(owner, carry):
        here = pl.ds(pl.multiple_of(owner * size, TILE), size)
        there = pl.ds(pl.multiple_of(owner * rows + at, TILE), size)
        pltpu.make_async_copy(ref.at[here], result.at[there], sem).start()
        return carry

    lax.fori_loop(0, n, body, 0)


def gather_rest_kernel(n, units, stages, rows, own, mid, high, link_send, link_recv):
    me = lax.axis_index("shard")
    quarter = rows // 4

    def place(u, owner):
        at = units[u][1]
        if at < rows // 2 + quarter:
            return mid, owner * quarter + at - rows // 2
        return high, owner * quarter + at - rows // 2 - quarter

    barrier = pltpu.get_barrier_semaphore()
    ladder = Ladder(n, units, stages[0][1], place, high, link_send, link_recv)
    has = (ladder.z >= 1, ladder.z <= ladder.last - 1, ladder.z >= 0)
    for way in range(3):

        @pl.when(has[way])
        def _(way=way):
            pl.semaphore_signal(
                barrier, inc=1, device_id={"shard": ladder.targets[way]}, device_id_type=MESH
            )

    group = loop_rows(quarter, own.shape[1])
    for j, ref in enumerate((mid, high)):

        def keep(r, carry, j=j, ref=ref):
            here = pl.ds(pl.multiple_of(j * quarter + r * group, TILE), group)
            there = pl.ds(pl.multiple_of(me * quarter + r * group, TILE), group)
            ref[there, :] = own[here, :]
            return carry

        lax.fori_loop(0, quarter // group, keep, 0)
    peers = 1 + has[DOWN].astype(jnp.int32) + has[UP].astype(jnp.int32)
    pl.semaphore_wait(barrier, peers)

    def body(c):
        halves = stages[c][1]
        ladder = Ladder(n, units, halves, place, high, link_send, link_recv)
        for u in halves[0] + halves[1]:
            ladder.send_own(u)
        ladder.run()
        ladder.finish()

    by_core(len(stages), body)


def write_rest_kernel(n, kinds, rows, partial, mid, high, result, sems):
    del partial
    spread(n, rows, high, result, 3 * rows // 4, sems.at[0])

    def more(c):
        if c == 0:
            spread(n, rows, mid, result, rows // 2, sems.at[1])
            pltpu.make_async_copy(mid, mid, sems.at[1]).wait()

    by_core(kinds, more)
    pltpu.make_async_copy(high, high, sems.at[0]).wait()


def local(
    n,
    width,
    w_query,
    first_query,
    second_query,
    w_key,
    first_key,
    second_key,
    w_value,
    first_value,
    second_value,
    norm_train,
    norm_step,
):
    groups = ((w_query, first_query, second_query), (w_key, first_key, second_key), (w_value, first_value, second_value))
    rows = w_query.shape[0]
    extents = [each[0].shape[1] for each in groups]
    units = plan_units(rows, extents)
    stages = plan_stages(units, extents)
    kinds = len(stages)
    piece = norm_train.shape[0]
    depth = n // 2
    dma = pltpu.SemaphoreType.DMA
    vmem = pl.BlockSpec(memory_space=pltpu.VMEM)
    hbm = pl.BlockSpec(memory_space=pltpu.HBM)
    serving = [jax.ShapeDtypeStruct((rows * n, e), jnp.bfloat16) for e in extents]
    whole = [jax.ShapeDtypeStruct((rows, e), jnp.float32) for e in extents]
    column = [jax.ShapeDtypeStruct((1, e), jnp.float32) for e in extents]
    wide = extents[0]
    half, quarter = (jax.ShapeDtypeStruct((n * rows // k, wide), jnp.bfloat16) for k in (2, 4))
    links = [dma((3, depth, 2)), dma((3, depth, 2))]
    gathered = pl.pallas_call(
        functools.partial(gather_kernel, n, width, units, stages),
        out_shape=[half, serving[1], serving[2], quarter, *whole, *column]
        + [jax.ShapeDtypeStruct((n, width, 1, piece), jnp.float32)],
        in_specs=[hbm] * 11,
        out_specs=[vmem] * 11,
        scratch_shapes=[pltpu.VMEM((3, rows, e), jnp.float32) for e in extents]
        + [pltpu.VMEM((n, 1, e), jnp.float32) for e in extents]
        + [
            pltpu.VMEM((2, 1, piece), jnp.float32),
            dma(()),
            dma((len(units),)),
            dma((3,)),
            dma((3,)),
            dma(()),
            dma(()),
            dma(()),
            dma(()),
            *links,
        ],
        compiler_params=pltpu.CompilerParams(
            collective_id=0, has_side_effects=True, vmem_limit_bytes=16 * 1024 * 1024
        ),
    )(
        *[pltpu.with_memory_space_constraint(each, pltpu.HBM) for group in groups for each in group],
        pltpu.with_memory_space_constraint(norm_train.reshape(1, -1), pltpu.HBM),
        pltpu.with_memory_space_constraint(norm_step.reshape(1, -1), pltpu.HBM),
    )
    gain = gathered[-1].reshape(-1, 128)
    partial, *written, own = pl.pallas_call(
        functools.partial(write_first_kernel, n, kinds),
        out_shape=[*serving, *whole, *column]
        + [jax.ShapeDtypeStruct(gain.shape, jnp.bfloat16)]
        + [jax.ShapeDtypeStruct((rows // 2, wide), jnp.bfloat16)],
        in_specs=[vmem] * 11,
        out_specs=[hbm] * 10 + [vmem],
        scratch_shapes=[pltpu.VMEM(gain.shape, jnp.bfloat16), dma((11,))],
        compiler_params=pltpu.CompilerParams(vmem_limit_bytes=16 * 1024 * 1024),
    )(*gathered[:-1], gain)
    mid, high = pl.pallas_call(
        functools.partial(gather_rest_kernel, n, units, stages, rows),
        out_shape=[quarter, quarter],
        in_specs=[vmem],
        out_specs=[vmem] * 2,
        scratch_shapes=links,
        compiler_params=pltpu.CompilerParams(
            collective_id=1, has_side_effects=True, vmem_limit_bytes=16 * 1024 * 1024
        ),
    )(own)
    serving_query = pl.pallas_call(
        functools.partial(write_rest_kernel, n, kinds, rows),
        out_shape=serving[0],
        in_specs=[hbm, vmem, vmem],
        out_specs=hbm,
        input_output_aliases={0: 0},
        scratch_shapes=[dma((2,))],
        compiler_params=pltpu.CompilerParams(vmem_limit_bytes=16 * 1024 * 1024),
    )(pltpu.with_memory_space_constraint(partial, pltpu.HBM), mid, high)
    serving_key, serving_value, *rest, norm = written
    wholes, columns = rest[:3], rest[3:]
    return (
        serving_query,
        serving_key,
        serving_value,
        *[each.reshape(-1) for each in columns],
        norm.reshape(-1),
        *wholes,
    )


def solution(mesh):
    split = P("shard", "width")
    both = P(("shard", "width"))
    n, width = mesh.shape["shard"], mesh.shape["width"]
    return jax.shard_map(
        functools.partial(local, n, width),
        mesh=mesh,
        in_specs=(split,) * 9 + (both, both),
        out_specs=(P(None, "width"),) * 3 + (P("width"),) * 3 + (P(),) + (split,) * 3,
        check_vma=False,
    )
```

time: 136 us -> 133 us (0.978)
  Pallas kernels: 135 us -> 132 us
    pallas_call x2 -> x4, Pallas kernels: 135 us -> 132 us  [the longest x1 91.1 us: local(): pl.pallas_call(functools.partial(gather_kernel, n, width, units, stages),...]
where the time goes in v4:
time: 133 us; the launch traced here: 132 us
  Pallas kernels  132 us (99%)
    pallas_call x1, Pallas kernels, local(): pl.pallas_call(functools.partial(gather_kernel, n, width, units, stages),...  91.1 us
    pallas_call x1, Pallas kernels, local(): pl.pallas_call(functools.partial(gather_rest_kernel, n, units, stages, ro...  34.3 us
    pallas_call x1, Pallas kernels, local(): pl.pallas_call(functools.partial(write_first_kernel, n, kinds), out_shape...  4.34 us

profile of v4, /device:TPU:0, one launch (start us, length us, event | category | flops | bytes accessed | tf_op | source)
XLA Modules:
  0.0 132.5 jit_solution(6599997933514965850)
XLA Ops:
  0.6 91.1 %shard_map.186 = (bf16[2048,1024]{1,0:T(8,128)(2,1)S(1)}, bf16[4096,256]{1,0:T(8,128)(2,1)S(1)}, bf16[4096,256]{1,0:T(8,128)(2,1)S(1)}, bf16[1024,1024]{1,0:T(8,...) custom-call(f32[512,1024]{1,0:T(8,128)} %w_q.1, ...), custom_call_target="tpu_custom_call" | custom-call | tf_op jit(solution)/shard_map/pallas_call | solution.py:613
  91.8 4.3 %shard_map.187 = (bf16[4096,1024]{1,0:T(8,128)(2,1)}, bf16[4096,256]{1,0:T(8,128)(2,1)}, bf16[4096,256]{1,0:T(8,128)(2,1)}, f32[512,1024]{1,0:T(8,128)}, f32[512...) custom-call(bf16[2048,1024]{1,0:T(8,128)(2,1)S(1)} %get-tuple-elemen, ...), custom_call_target="tpu_custom_call" | custom-call | tf_op jit(solution)/shard_map/pallas_call | solution.py:642
  96.1 34.3 %shard_map.188 = (bf16[1024,1024]{1,0:T(8,128)(2,1)S(1)}, bf16[1024,1024]{1,0:T(8,128)(2,1)S(1)}) custom-call(bf16[256,1024]{1,0:T(8,128)(2,1)S(1)} %get-tuple-element.46.own), custom_call_target="tpu_custom_call" | custom-call | tf_op jit(solution)/shard_map/pallas_call | solution.py:652
  130.4 2.0 %shard_map.189 = bf16[4096,1024]{1,0:T(8,128)(2,1)} custom-call(bf16[4096,1024]{1,0:T(8,128)(2,1)} %get-tuple-element.45.partial, bf16[1024,1024]{1,0:T(8,128)(2,1)S(1)} %get-tuple-element.47.mid, bf16[1024,1024]{1,0:T(8,128)(2,1)S(1)} %get-tuple-element.48.high), custom_call_target="tpu_custom_call", output_to_operand_aliasing={{}: (0, {})} | custom-call | tf_op jit(solution)/shard_map/pallas_call | solution.py:662

commit v5 on v4

--- a/solution.py
+++ b/solution.py
@@ -13,13 +13,24 @@
 MESH = pl.DeviceIdType.MESH
 TILE = 16
 DOWN, UP, CROSS = 0, 1, 2
+CUTS = (0.75, 0.5)
+LATER = CUTS.index(max(CUTS))
 
 
 def plan_units(rows, extents):
     wide = extents.index(max(extents))
     units = [(i, 0, rows) for i in range(len(extents)) if i != wide]
-    count = 8 if rows % (8 * TILE) == 0 else 4
+    early = max(TILE, rows // 4)
+    units[:1] = [(units[0][0], 0, early), (units[0][0], early, rows - early)]
+    count = math.gcd(16, rows // TILE)
     return units + [(wide, j * (rows // count), rows // count) for j in range(count)]
+
+
+def plan_loads(units, rows):
+    wide = units[-1][0]
+    count = math.gcd(4, rows // TILE)
+    others = dict.fromkeys(unit[0] for unit in units if unit[0] != wide)
+    return [(i, 0, rows) for i in others] + [(wide, j * (rows // count), rows // count) for j in range(count)]
 
 
 def plan_stages(units, extents):
@@ -27,14 +38,16 @@
     narrow = [u for u, unit in enumerate(units) if unit[0] != wide]
     rest = [u for u, unit in enumerate(units) if unit[0] == wide]
     count = len(rest)
-    cuts = (count // 2, 3 * count // 4) if count >= 8 else (count // 2,)
+    cuts = tuple(round(count * cut) for cut in CUTS) if count >= 16 else (count // 2,)
 
     def split(chosen):
         sizes = [extents[units[u][0]] * units[u][2] for u in chosen]
         at = min(range(1, len(chosen)), key=lambda k: abs(2 * sum(sizes[:k]) - sum(sizes)))
         return chosen[:at], chosen[at:]
 
-    return [(split(narrow + rest[:cut]), split(rest[cut:])) for cut in cuts]
+    size = units[-1][2]
+    stages = [(split(narrow + rest[:cut]), split(rest[cut:])) for cut in cuts]
+    return stages, min(cuts) * size, max(cuts) * size
 
 
 def loop_rows(size, extent):
@@ -42,7 +55,8 @@
 
 
 class Ladder:
-    def __init__(self, n, units, halves, place, spare, link_send, link_recv):
+    def __init__(self, n, units, halves, place, spare, link_send, link_recv, early=None):
+        self.early = early
         self.depth, self.units, self.halves, self.place, self.spare = n // 2, units, halves, place, spare
         self.link_send, self.link_recv = link_send, link_recv
         me = lax.axis_index("shard")
@@ -62,7 +76,8 @@
         )
 
     def bundle(self, g, way, slot):
-        words = sum(self.units[u][2] * self.place(u, 0)[0].shape[1] for u in self.halves[g])
+        there = [u for u in self.halves[g] if not (self.early and u == 0 and isinstance(slot, int) and slot == 0)]
+        words = sum(self.units[u][2] * self.place(u, 0)[0].shape[1] for u in there)
         ref = self.spare.at[pl.ds(0, words // self.spare.shape[1])]
         return self.joint(ref, self.link_send.at[way, slot, g], self.link_recv.at[way, slot, g])
 
@@ -125,8 +140,11 @@
         z, x, depth, last = self.z, self.x, self.depth, self.last
         for g in range(2):
 
+            before = self.early if self.early and g == 0 and isinstance(t, int) else lambda way, owner: None
+
             @pl.when(z + t <= last)
-            def _(g=g):
+            def _(g=g, before=before):
+                before(DOWN, (z + t) * 2 + x)
                 self.bundle(g, DOWN, t - 1).wait_recv()
 
                 @pl.when(z >= 1)
@@ -136,7 +154,8 @@
                 self.across(z + t, g, t, (z == 1) & (z + t == last))
 
             @pl.when(z - t >= 0)
-            def _(g=g):
+            def _(g=g, before=before):
+                before(UP, (z - t) * 2 + x)
                 self.bundle(g, UP, t - 1).wait_recv()
 
                 @pl.when(z <= depth - 2)
@@ -145,7 +164,11 @@
 
                 self.across(z - t, g, depth - t, (z == depth - 2) & (z == t))
 
-            @pl.when((t == 1) & (self.low_end | self.high_end))
+            if not isinstance(t, int):
+                continue
+            before(CROSS, z * 2 + 1 - x)
+
+            @pl.when(self.low_end | self.high_end)
             def _(g=g):
                 self.bundle(g, CROSS, 0).wait_recv()
 
@@ -170,7 +193,8 @@
         return carry
 
     def run(self):
-        lax.fori_loop(1, self.depth, self.step, 0)
+        self.step(1, 0)
+        lax.fori_loop(2, self.depth, self.step, 0)
 
     def finish(self):
         z, depth, last = self.z, self.depth, self.last
@@ -193,10 +217,10 @@
                 def _(g=g):
                     self.bundle(g, UP, t).wait_send()
 
-                for source, slot, there in (
-                    (above, t, above <= last),
-                    (below, depth - t, (t > 0) & (below >= 0)),
-                ):
+                both = [(above, t, above <= last)]
+                if not isinstance(t, int):
+                    both.append((below, depth - t, below >= 0))
+                for source, slot, there in both:
 
                     @pl.when(there & self.crosses(source, g))
                     def _(g=g, slot=slot):
@@ -208,7 +232,8 @@
 
             return carry
 
-        lax.fori_loop(0, depth, rest, 0)
+        rest(0, 0)
+        lax.fori_loop(1, depth, rest, 0)
         for g in range(2):
             to_above, to_below = self.low_end, self.high_end
             from_above = (z >= depth // 2) & (z <= depth - 2)
@@ -260,8 +285,10 @@
 def gather_kernel(
     n,
     width,
+    chunks,
     units,
     stages,
+    cut,
     w_q,
     first_q,
     second_q,
@@ -291,6 +318,9 @@
     sums_k,
     sums_v,
     in_norm,
+    in_early,
+    early_send,
+    early_recv,
     norm_sem,
     load_sem,
     sum_send,
@@ -308,8 +338,31 @@
     staged, sums = (in_q, in_k, in_v), (sums_q, sums_k, sums_v)
     sources = ((w_q, first_q, second_q), (w_k, first_k, second_k), (w_v, first_v, second_v))
     rows = whole_q.shape[0]
-    count = len(units)
     order = list(dict.fromkeys(unit[0] for unit in units))
+
+    loads = []
+    for u, (i, at, size) in enumerate(chunks):
+        group = []
+        for j in range(3):
+            copy = pltpu.make_async_copy(
+                sources[i][j].at[pl.ds(at, size)], staged[i].at[j, pl.ds(at, size)], load_sem.at[u]
+            )
+            group.append(copy)
+        loads.append(group)
+
+    def load(array_is_first):
+        for (i, _, _), group in zip(chunks, loads):
+            if (i == order[0]) == array_is_first:
+                for copy in group:
+                    copy.start()
+
+    load(True)
+    norm_loads = [
+        pltpu.make_async_copy(ref, in_norm.at[j], norm_sem)
+        for j, ref in enumerate((norm_train, norm_step))
+    ]
+    for copy in norm_loads:
+        copy.start()
 
     barrier = pltpu.get_barrier_semaphore()
     for k in range(1, n):
@@ -321,34 +374,30 @@
             barrier, inc=1, device_id={"width": lax.rem(me_w + k, width)}, device_id_type=MESH
         )
 
-    loads = []
-    for u, (i, at, size) in enumerate(units):
-        group = []
-        for j in range(3):
-            copy = pltpu.make_async_copy(
-                sources[i][j].at[pl.ds(at, size)], staged[i].at[j, pl.ds(at, size)], load_sem.at[u]
-            )
-            group.append(copy)
-        loads.append(group)
-
-    def load(array_is_first):
-        for (i, _, _), group in zip(units, loads):
-            if (i == order[0]) == array_is_first:
-                for copy in group:
-                    copy.start()
-
-    load(True)
-    norm_loads = [
-        pltpu.make_async_copy(ref, in_norm.at[j], norm_sem)
-        for j, ref in enumerate((norm_train, norm_step))
-    ]
-    for copy in norm_loads:
-        copy.start()
-
     first = units[0][0]
 
+    z, x = lax.div(me, 2), lax.rem(me, 2)
+    last = n // 2 - 1
+    targets = (lax.max(z - 1, 0) * 2 + x, lax.min(z + 1, last) * 2 + x, z * 2 + 1 - x)
+    has = (z >= 1, z <= last - 1, z >= 0)
+
+    def early(way):
+        return pltpu.make_async_remote_copy(
+            src_ref=wholes[first].at[pl.ds(0, units[0][2])],
+            dst_ref=in_early.at[way],
+            send_sem=early_send.at[way],
+            recv_sem=early_recv.at[way],
+            device_id={"shard": targets[way]},
+            device_id_type=MESH,
+        )
+
+    def early_arrived(way, owner):
+        early(way).wait_recv()
+        ref, there = place(0, owner)
+        scaled(in_early.at[way], 0, ref, there, units[0][2], 1.0 / cols[first][...])
+
     def block_sums(u, total):
-        i, at, size = units[u]
+        i, at, size = chunks[u]
         stage, whole = staged[i], wholes[i]
         group = loop_rows(size, whole.shape[1])
 
@@ -363,10 +412,10 @@
         return lax.fori_loop(0, size // group, update, total)
 
     for i in order:
-        mine = [u for u in range(count) if units[u][0] == i]
+        mine = [u for u in range(len(chunks)) if chunks[u][0] == i]
         total = jnp.zeros((8, wholes[i].shape[1]), jnp.float32)
         for u in mine:
-            _, at, size = units[u]
+            _, at, size = chunks[u]
             whole_load = staged[i].at[:, pl.ds(at, size)]
             pltpu.make_async_copy(whole_load, whole_load, load_sem.at[u]).wait()
             if u == 0:
@@ -385,6 +434,9 @@
                 device_id_type=MESH,
             )
             copy.start()
+        if i == order[min(1, len(order) - 1)]:
+            for way in range(3):
+                pl.when(has[way])(lambda way=way: early(way).start())
         if i == first:
             pltpu.make_async_copy(in_norm, in_norm, norm_sem).wait()
             norm_out[me, me_w] = in_norm[0] + in_norm[1]
@@ -403,14 +455,14 @@
         i, at, _ = units[u]
         if i == 1 or i == 2:
             return (out_k, out_v)[i - 1], owner * rows + at
-        if at < rows // 2:
-            return low, owner * (rows // 2) + at
-        return mid, owner * (rows // 4) + at - rows // 2
+        if at < cut[0]:
+            return low, owner * cut[0] + at
+        return mid, owner * (cut[1] - cut[0]) + at - cut[0]
 
     def body(c):
         halves = stages[c][0]
         mine = halves[0] + halves[1]
-        ladder = Ladder(n, units, halves, place, low, link_send, link_recv)
+        ladder = Ladder(n, units, halves, place, out_k, link_send, link_recv, early_arrived)
         for i in order:
             ladder.joint(sums[i].at[pl.ds(0, n - 1)], sum_send.at[i], sum_recv.at[i]).wait_recv()
             total = sums[i][0]
@@ -423,8 +475,12 @@
                 owner, at, size = units[u]
                 if owner == i:
                     ref, there = place(u, me)
-                    scaled(wholes[i], at, ref, there, size, factor)
-                    ladder.send_own(u)
+                    if u > 0:
+                        scaled(wholes[i], at, ref, there, size, factor)
+                        ladder.send_own(u)
+            if i == first:
+                ref, there = place(0, me)
+                scaled(wholes[i], 0, ref, there, units[0][2], factor)
         ladder.joint(norm_out.at[0, pl.ds(0, width - 1)], wid_send, wid_recv).wait_recv()
         for k in range(1, n):
             pltpu.make_async_remote_copy(
@@ -440,6 +496,8 @@
         for i in order:
             ladder.joint(sums[i].at[pl.ds(0, n - 1)], sum_send.at[i], sum_recv.at[i]).wait_send()
         ladder.joint(norm_out.at[pl.ds(0, n - 1)], nrm_send, nrm_recv).wait()
+        for way in range(3):
+            pl.when(has[way])(lambda way=way: early(way).wait_send())
         ladder.finish()
 
     by_core(len(stages), body)
@@ -448,6 +506,7 @@
 def write_first_kernel(
     n,
     kinds,
+    cut,
     low,
     out_k,
     out_v,
@@ -489,16 +548,16 @@
     spread(n, rows, low, to_q, 0, sems.at[8])
 
     def more(c):
-        if c == 1:
-            spread(n, rows, mid, to_q, rows // 2, sems.at[9])
+        if kinds > 1 and c == LATER:
+            spread(n, rows, mid, to_q, cut[0], sems.at[9])
 
     by_core(kinds, more)
     norm[...] = norm_in[...].astype(jnp.bfloat16)
     pltpu.make_async_copy(norm, to_norm, sems.at[10]).start()
-    scaled(whole_q, rows // 2, own, 0, rows // 2, 1.0 / col_q[...])
+    scaled(whole_q, cut[0], own, 0, rows - cut[0], 1.0 / col_q[...])
 
     def end(c):
-        if c == 1:
+        if kinds > 1 and c == LATER:
             pltpu.make_async_copy(mid, mid, sems.at[9]).wait()
 
     for j, (ref, result) in enumerate(pairs):
@@ -520,15 +579,15 @@
     lax.fori_loop(0, n, body, 0)
 
 
-def gather_rest_kernel(n, units, stages, rows, own, mid, high, link_send, link_recv):
+def gather_rest_kernel(n, units, stages, cut, rows, own, mid, high, link_send, link_recv):
     me = lax.axis_index("shard")
-    quarter = rows // 4
+    start, end = cut
 
     def place(u, owner):
         at = units[u][1]
-        if at < rows // 2 + quarter:
-            return mid, owner * quarter + at - rows // 2
-        return high, owner * quarter + at - rows // 2 - quarter
+        if at < end:
+            return mid, owner * (end - start) + at - start
+        return high, owner * (rows - end) + at - end
 
     barrier = pltpu.get_barrier_semaphore()
     ladder = Ladder(n, units, stages[0][1], place, high, link_send, link_recv)
@@ -541,16 +600,17 @@
                 barrier, inc=1, device_id={"shard": ladder.targets[way]}, device_id_type=MESH
             )
 
-    group = loop_rows(quarter, own.shape[1])
-    for j, ref in enumerate((mid, high)):
-
-        def keep(r, carry, j=j, ref=ref):
-            here = pl.ds(pl.multiple_of(j * quarter + r * group, TILE), group)
-            there = pl.ds(pl.multiple_of(me * quarter + r * group, TILE), group)
+    for ref, at, size in ((mid, 0, end - start), (high, end - start, rows - end)):
+        group = math.gcd(loop_rows(size, own.shape[1]), at)
+
+        def keep(r, carry, ref=ref, at=at, size=size, group=group):
+            here = pl.ds(pl.multiple_of(at + r * group, TILE), group)
+            there = pl.ds(pl.multiple_of(me * size + r * group, TILE), group)
             ref[there, :] = own[here, :]
             return carry
 
-        lax.fori_loop(0, quarter // group, keep, 0)
+        if size:
+            lax.fori_loop(0, size // group, keep, 0)
     peers = 1 + has[DOWN].astype(jnp.int32) + has[UP].astype(jnp.int32)
     pl.semaphore_wait(barrier, peers)
 
@@ -565,13 +625,13 @@
     by_core(len(stages), body)
 
 
-def write_rest_kernel(n, kinds, rows, partial, mid, high, result, sems):
+def write_rest_kernel(n, kinds, cut, rows, partial, mid, high, result, sems):
     del partial
-    spread(n, rows, high, result, 3 * rows // 4, sems.at[0])
+    spread(n, rows, high, result, cut[1], sems.at[0])
 
     def more(c):
-        if c == 0:
-            spread(n, rows, mid, result, rows // 2, sems.at[1])
+        if kinds > 1 and c != LATER:
+            spread(n, rows, mid, result, cut[0], sems.at[1])
             pltpu.make_async_copy(mid, mid, sems.at[1]).wait()
 
     by_core(kinds, more)
@@ -597,7 +657,8 @@
     rows = w_query.shape[0]
     extents = [each[0].shape[1] for each in groups]
     units = plan_units(rows, extents)
-    stages = plan_stages(units, extents)
+    stages, *cut = plan_stages(units, extents)
+    chunks = plan_loads(units, rows)
     kinds = len(stages)
     piece = norm_train.shape[0]
     depth = n // 2
@@ -608,11 +669,14 @@
     whole = [jax.ShapeDtypeStruct((rows, e), jnp.float32) for e in extents]
     column = [jax.ShapeDtypeStruct((1, e), jnp.float32) for e in extents]
     wide = extents[0]
-    half, quarter = (jax.ShapeDtypeStruct((n * rows // k, wide), jnp.bfloat16) for k in (2, 4))
+    low, mid, high = (
+        jax.ShapeDtypeStruct((n * max(size, TILE), wide), jnp.bfloat16)
+        for size in (cut[0], cut[1] - cut[0], rows - cut[1])
+    )
     links = [dma((3, depth, 2)), dma((3, depth, 2))]
     gathered = pl.pallas_call(
-        functools.partial(gather_kernel, n, width, units, stages),
-        out_shape=[half, serving[1], serving[2], quarter, *whole, *column]
+        functools.partial(gather_kernel, n, width, chunks, units, stages, cut),
+        out_shape=[low, serving[1], serving[2], mid, *whole, *column]
         + [jax.ShapeDtypeStruct((n, width, 1, piece), jnp.float32)],
         in_specs=[hbm] * 11,
         out_specs=[vmem] * 11,
@@ -620,8 +684,11 @@
         + [pltpu.VMEM((n, 1, e), jnp.float32) for e in extents]
         + [
             pltpu.VMEM((2, 1, piece), jnp.float32),
+            pltpu.VMEM((3, units[0][2], extents[units[0][0]]), jnp.float32),
+            dma((3,)),
+            dma((3,)),
             dma(()),
-            dma((len(units),)),
+            dma((len(chunks),)),
             dma((3,)),
             dma((3,)),
             dma(()),
@@ -640,18 +707,18 @@
     )
     gain = gathered[-1].reshape(-1, 128)
     partial, *written, own = pl.pallas_call(
-        functools.partial(write_first_kernel, n, kinds),
+        functools.partial(write_first_kernel, n, kinds, cut),
         out_shape=[*serving, *whole, *column]
         + [jax.ShapeDtypeStruct(gain.shape, jnp.bfloat16)]
-        + [jax.ShapeDtypeStruct((rows // 2, wide), jnp.bfloat16)],
+        + [jax.ShapeDtypeStruct((rows - cut[0], wide), jnp.bfloat16)],
         in_specs=[vmem] * 11,
         out_specs=[hbm] * 10 + [vmem],
         scratch_shapes=[pltpu.VMEM(gain.shape, jnp.bfloat16), dma((11,))],
         compiler_params=pltpu.CompilerParams(vmem_limit_bytes=16 * 1024 * 1024),
     )(*gathered[:-1], gain)
     mid, high = pl.pallas_call(
-        functools.partial(gather_rest_kernel, n, units, stages, rows),
-        out_shape=[quarter, quarter],
+        functools.partial(gather_rest_kernel, n, units, stages, cut, rows),
+        out_shape=[mid, high],
         in_specs=[vmem],
         out_specs=[vmem] * 2,
         scratch_shapes=links,
@@ -660,7 +727,7 @@
         ),
     )(own)
     serving_query = pl.pallas_call(
-        functools.partial(write_rest_kernel, n, kinds, rows),
+        functools.partial(write_rest_kernel, n, kinds, cut, rows),
         out_shape=serving[0],
         in_specs=[hbm, vmem, vmem],
         out_specs=hbm,

time: 133 us -> 131 us (0.985)
  Pallas kernels: 132 us -> 130 us
    pallas_call x4, Pallas kernels: 132 us -> 130 us  [the longest x1 102 us: local(): pl.pallas_call(functools.partial(gather_kernel, n, width, chunks, units,...]
where the time goes in v5:
time: 131 us
  Pallas kernels  130 us (99%)
    pallas_call x1, Pallas kernels, local(): pl.pallas_call(functools.partial(gather_kernel, n, width, chunks, units,...  102 us
    pallas_call x1, Pallas kernels, local(): pl.pallas_call(functools.partial(gather_rest_kernel, n, units, stages, cu...  22.2 us
    pallas_call x1, Pallas kernels, local(): pl.pallas_call(functools.partial(write_first_kernel, n, kinds, cut), out_...  4.96 us

profile of v5, /device:TPU:0, one launch (start us, length us, event | category | flops | bytes accessed | tf_op | source)
XLA Modules:
  0.0 130.9 jit_solution(2244261527758638925)
XLA Ops:
  0.6 101.7 %shard_map.186 = (bf16[2048,1024]{1,0:T(8,128)(2,1)S(1)}, bf16[4096,256]{1,0:T(8,128)(2,1)S(1)}, bf16[4096,256]{1,0:T(8,128)(2,1)S(1)}, bf16[1024,1024]{1,0:T(8,...) custom-call(f32[512,1024]{1,0:T(8,128)} %w_q.1, ...), custom_call_target="tpu_custom_call" | custom-call | tf_op jit(solution)/shard_map/pallas_call | solution.py:677
  102.4 5.0 %shard_map.187 = (bf16[4096,1024]{1,0:T(8,128)(2,1)}, bf16[4096,256]{1,0:T(8,128)(2,1)}, bf16[4096,256]{1,0:T(8,128)(2,1)}, f32[512,1024]{1,0:T(8,128)}, f32[512...) custom-call(bf16[2048,1024]{1,0:T(8,128)(2,1)S(1)} %get-tuple-elemen, ...), custom_call_target="tpu_custom_call" | custom-call | tf_op jit(solution)/shard_map/pallas_call | solution.py:709
  107.4 22.2 %shard_map.188 = (bf16[1024,1024]{1,0:T(8,128)(2,1)S(1)}, bf16[1024,1024]{1,0:T(8,128)(2,1)S(1)}) custom-call(bf16[256,1024]{1,0:T(8,128)(2,1)S(1)} %get-tuple-element.46.own), custom_call_target="tpu_custom_call" | custom-call | tf_op jit(solution)/shard_map/pallas_call | solution.py:719
  129.6 1.3 %shard_map.189 = bf16[4096,1024]{1,0:T(8,128)(2,1)} custom-call(bf16[4096,1024]{1,0:T(8,128)(2,1)} %get-tuple-element.45.partial, bf16[1024,1024]{1,0:T(8,128)(2,1)S(1)} %get-tuple-element.47.mid, bf16[1024,1024]{1,0:T(8,128)(2,1)S(1)} %get-tuple-element.48.high), custom_call_target="tpu_custom_call", output_to_operand_aliasing={{}: (0, {})} | custom-call | tf_op jit(solution)/shard_map/pallas_call | solution.py:729

commit v6 on v5

--- a/solution.py
+++ b/solution.py
@@ -319,17 +319,12 @@
     sums_v,
     in_norm,
     in_early,
-    early_send,
     early_recv,
     norm_sem,
     load_sem,
-    sum_send,
     sum_recv,
-    wid_send,
     wid_recv,
-    nrm_send,
     nrm_recv,
-    link_send,
     link_recv,
 ):
     me = lax.axis_index("shard")
@@ -340,6 +335,16 @@
     rows = whole_q.shape[0]
     order = list(dict.fromkeys(unit[0] for unit in units))
 
+    barrier = pltpu.get_barrier_semaphore()
+    for k in range(1, n):
+        pl.semaphore_signal(
+            barrier, inc=1, device_id={"shard": lax.rem(me + k, n)}, device_id_type=MESH
+        )
+    for k in range(1, width):
+        pl.semaphore_signal(
+            barrier, inc=1, device_id={"width": lax.rem(me_w + k, width)}, device_id_type=MESH
+        )
+
     loads = []
     for u, (i, at, size) in enumerate(chunks):
         group = []
@@ -364,143 +369,138 @@
     for copy in norm_loads:
         copy.start()
 
-    barrier = pltpu.get_barrier_semaphore()
-    for k in range(1, n):
-        pl.semaphore_signal(
-            barrier, inc=1, device_id={"shard": lax.rem(me + k, n)}, device_id_type=MESH
-        )
-    for k in range(1, width):
-        pl.semaphore_signal(
-            barrier, inc=1, device_id={"width": lax.rem(me_w + k, width)}, device_id_type=MESH
-        )
-
-    first = units[0][0]
-
-    z, x = lax.div(me, 2), lax.rem(me, 2)
-    last = n // 2 - 1
-    targets = (lax.max(z - 1, 0) * 2 + x, lax.min(z + 1, last) * 2 + x, z * 2 + 1 - x)
-    has = (z >= 1, z <= last - 1, z >= 0)
-
-    def early(way):
-        return pltpu.make_async_remote_copy(
-            src_ref=wholes[first].at[pl.ds(0, units[0][2])],
-            dst_ref=in_early.at[way],
-            send_sem=early_send.at[way],
-            recv_sem=early_recv.at[way],
-            device_id={"shard": targets[way]},
-            device_id_type=MESH,
-        )
-
-    def early_arrived(way, owner):
-        early(way).wait_recv()
-        ref, there = place(0, owner)
-        scaled(in_early.at[way], 0, ref, there, units[0][2], 1.0 / cols[first][...])
-
-    def block_sums(u, total):
-        i, at, size = chunks[u]
-        stage, whole = staged[i], wholes[i]
-        group = loop_rows(size, whole.shape[1])
-
-        def update(r, total):
-            for j in range(group // 8):
-                here = pl.ds(pl.multiple_of(at + r * group + j * 8, 8), 8)
-                new = stage[0, here] - learn_rate * (hold_rate * stage[1, here] + stage[2, here])
-                whole[here, :] = new
-                total = total + jnp.abs(new)
-            return total
-
-        return lax.fori_loop(0, size // group, update, total)
-
-    for i in order:
-        mine = [u for u in range(len(chunks)) if chunks[u][0] == i]
-        total = jnp.zeros((8, wholes[i].shape[1]), jnp.float32)
-        for u in mine:
-            _, at, size = chunks[u]
-            whole_load = staged[i].at[:, pl.ds(at, size)]
-            pltpu.make_async_copy(whole_load, whole_load, load_sem.at[u]).wait()
-            if u == 0:
-                load(False)
-            total = block_sums(u, total)
-        sums[i][me] = jnp.sum(total, axis=0, keepdims=True)
-        if i == first:
-            pl.semaphore_wait(barrier, n - 1 + width - 1)
-        for k in range(1, n):
-            copy = pltpu.make_async_remote_copy(
-                src_ref=sums[i].at[me],
-                dst_ref=sums[i].at[me],
-                send_sem=sum_send.at[i],
-                recv_sem=sum_recv.at[i],
-                device_id={"shard": lax.rem(me + k, n)},
+    dma = pltpu.SemaphoreType.DMA
+
+    def main(early_send, sum_send, wid_send, nrm_send, link_send):
+        first = units[0][0]
+
+        z, x = lax.div(me, 2), lax.rem(me, 2)
+        last = n // 2 - 1
+        targets = (lax.max(z - 1, 0) * 2 + x, lax.min(z + 1, last) * 2 + x, z * 2 + 1 - x)
+        has = (z >= 1, z <= last - 1, z >= 0)
+
+        def early(way):
+            return pltpu.make_async_remote_copy(
+                src_ref=wholes[first].at[pl.ds(0, units[0][2])],
+                dst_ref=in_early.at[way],
+                send_sem=early_send.at[way],
+                recv_sem=early_recv.at[way],
+                device_id={"shard": targets[way]},
                 device_id_type=MESH,
             )
-            copy.start()
-        if i == order[min(1, len(order) - 1)]:
-            for way in range(3):
-                pl.when(has[way])(lambda way=way: early(way).start())
-        if i == first:
-            pltpu.make_async_copy(in_norm, in_norm, norm_sem).wait()
-            norm_out[me, me_w] = in_norm[0] + in_norm[1]
-            for k in range(1, width):
+
+        def early_arrived(way, owner):
+            early(way).wait_recv()
+            ref, there = place(0, owner)
+            scaled(in_early.at[way], 0, ref, there, units[0][2], 1.0 / cols[first][...])
+
+        def block_sums(u, total):
+            i, at, size = chunks[u]
+            stage, whole = staged[i], wholes[i]
+            group = loop_rows(size, whole.shape[1])
+
+            def update(r, total):
+                for j in range(group // 8):
+                    here = pl.ds(pl.multiple_of(at + r * group + j * 8, 8), 8)
+                    new = stage[0, here] - learn_rate * (hold_rate * stage[1, here] + stage[2, here])
+                    whole[here, :] = new
+                    total = total + jnp.abs(new)
+                return total
+
+            return lax.fori_loop(0, size // group, update, total)
+
+        for i in order:
+            mine = [u for u in range(len(chunks)) if chunks[u][0] == i]
+            total = jnp.zeros((8, wholes[i].shape[1]), jnp.float32)
+            for u in mine:
+                _, at, size = chunks[u]
+                whole_load = staged[i].at[:, pl.ds(at, size)]
+                pltpu.make_async_copy(whole_load, whole_load, load_sem.at[u]).wait()
+                if u == 0:
+                    load(False)
+                total = block_sums(u, total)
+            sums[i][me] = jnp.sum(total, axis=0, keepdims=True)
+            if i == first:
+                pl.semaphore_wait(barrier, n - 1 + width - 1)
+            for k in range(1, n):
                 copy = pltpu.make_async_remote_copy(
-                    src_ref=norm_out.at[me, me_w],
-                    dst_ref=norm_out.at[me, me_w],
-                    send_sem=wid_send,
-                    recv_sem=wid_recv,
-                    device_id={"width": lax.rem(me_w + k, width)},
+                    src_ref=sums[i].at[me],
+                    dst_ref=sums[i].at[me],
+                    send_sem=sum_send.at[i],
+                    recv_sem=sum_recv.at[i],
+                    device_id={"shard": lax.rem(me + k, n)},
                     device_id_type=MESH,
                 )
                 copy.start()
-
-    def place(u, owner):
-        i, at, _ = units[u]
-        if i == 1 or i == 2:
-            return (out_k, out_v)[i - 1], owner * rows + at
-        if at < cut[0]:
-            return low, owner * cut[0] + at
-        return mid, owner * (cut[1] - cut[0]) + at - cut[0]
-
-    def body(c):
-        halves = stages[c][0]
-        mine = halves[0] + halves[1]
-        ladder = Ladder(n, units, halves, place, out_k, link_send, link_recv, early_arrived)
-        for i in order:
-            ladder.joint(sums[i].at[pl.ds(0, n - 1)], sum_send.at[i], sum_recv.at[i]).wait_recv()
-            total = sums[i][0]
+            if i == order[min(1, len(order) - 1)]:
+                for way in range(3):
+                    pl.when(has[way])(lambda way=way: early(way).start())
+            if i == first:
+                pltpu.make_async_copy(in_norm, in_norm, norm_sem).wait()
+                norm_out[me, me_w] = in_norm[0] + in_norm[1]
+                for k in range(1, width):
+                    copy = pltpu.make_async_remote_copy(
+                        src_ref=norm_out.at[me, me_w],
+                        dst_ref=norm_out.at[me, me_w],
+                        send_sem=wid_send,
+                        recv_sem=wid_recv,
+                        device_id={"width": lax.rem(me_w + k, width)},
+                        device_id_type=MESH,
+                    )
+                    copy.start()
+
+        def place(u, owner):
+            i, at, _ = units[u]
+            if i == 1 or i == 2:
+                return (out_k, out_v)[i - 1], owner * rows + at
+            if at < cut[0]:
+                return low, owner * cut[0] + at
+            return mid, owner * (cut[1] - cut[0]) + at - cut[0]
+
+        def body(c):
+            halves = stages[c][0]
+            mine = halves[0] + halves[1]
+            ladder = Ladder(n, units, halves, place, out_k, link_send, link_recv, early_arrived)
+            for i in order:
+                ladder.joint(sums[i].at[pl.ds(0, n - 1)], sum_send.at[i], sum_recv.at[i]).wait_recv()
+                total = sums[i][0]
+                for k in range(1, n):
+                    total = total + sums[i][k]
+                col = total / (rows * n)
+                cols[i][...] = col
+                factor = 1.0 / col
+                for u in mine:
+                    owner, at, size = units[u]
+                    if owner == i:
+                        ref, there = place(u, me)
+                        if u > 0:
+                            scaled(wholes[i], at, ref, there, size, factor)
+                            ladder.send_own(u)
+                if i == first:
+                    ref, there = place(0, me)
+                    scaled(wholes[i], 0, ref, there, units[0][2], factor)
+            ladder.joint(norm_out.at[0, pl.ds(0, width - 1)], wid_send, wid_recv).wait_recv()
             for k in range(1, n):
-                total = total + sums[i][k]
-            col = total / (rows * n)
-            cols[i][...] = col
-            factor = 1.0 / col
-            for u in mine:
-                owner, at, size = units[u]
-                if owner == i:
-                    ref, there = place(u, me)
-                    if u > 0:
-                        scaled(wholes[i], at, ref, there, size, factor)
-                        ladder.send_own(u)
-            if i == first:
-                ref, there = place(0, me)
-                scaled(wholes[i], 0, ref, there, units[0][2], factor)
-        ladder.joint(norm_out.at[0, pl.ds(0, width - 1)], wid_send, wid_recv).wait_recv()
-        for k in range(1, n):
-            pltpu.make_async_remote_copy(
-                src_ref=norm_out.at[me],
-                dst_ref=norm_out.at[me],
-                send_sem=nrm_send,
-                recv_sem=nrm_recv,
-                device_id={"shard": lax.rem(me + k, n)},
-                device_id_type=MESH,
-            ).start()
-        ladder.run()
-        ladder.joint(norm_out.at[0, pl.ds(0, width - 1)], wid_send, wid_recv).wait_send()
-        for i in order:
-            ladder.joint(sums[i].at[pl.ds(0, n - 1)], sum_send.at[i], sum_recv.at[i]).wait_send()
-        ladder.joint(norm_out.at[pl.ds(0, n - 1)], nrm_send, nrm_recv).wait()
-        for way in range(3):
-            pl.when(has[way])(lambda way=way: early(way).wait_send())
-        ladder.finish()
-
-    by_core(len(stages), body)
+                pltpu.make_async_remote_copy(
+                    src_ref=norm_out.at[me],
+                    dst_ref=norm_out.at[me],
+                    send_sem=nrm_send,
+                    recv_sem=nrm_recv,
+                    device_id={"shard": lax.rem(me + k, n)},
+                    device_id_type=MESH,
+                ).start()
+            ladder.run()
+            ladder.joint(norm_out.at[0, pl.ds(0, width - 1)], wid_send, wid_recv).wait_send()
+            for i in order:
+                ladder.joint(sums[i].at[pl.ds(0, n - 1)], sum_send.at[i], sum_recv.at[i]).wait_send()
+            ladder.joint(norm_out.at[pl.ds(0, n - 1)], nrm_send, nrm_recv).wait()
+            for way in range(3):
+                pl.when(has[way])(lambda way=way: early(way).wait_send())
+            ladder.finish()
+
+        by_core(len(stages), body)
+
+    pl.run_scoped(main, dma((3,)), dma((3,)), dma(()), dma(()), dma((3, n // 2, 2)))
 
 
 def write_first_kernel(
@@ -579,7 +579,7 @@
     lax.fori_loop(0, n, body, 0)
 
 
-def gather_rest_kernel(n, units, stages, cut, rows, own, mid, high, link_send, link_recv):
+def gather_rest_kernel(n, units, stages, cut, rows, own, mid, high, link_recv):
     me = lax.axis_index("shard")
     start, end = cut
 
@@ -590,7 +590,7 @@
         return high, owner * (rows - end) + at - end
 
     barrier = pltpu.get_barrier_semaphore()
-    ladder = Ladder(n, units, stages[0][1], place, high, link_send, link_recv)
+    ladder = Ladder(n, units, stages[0][1], place, high, None, link_recv)
     has = (ladder.z >= 1, ladder.z <= ladder.last - 1, ladder.z >= 0)
     for way in range(3):
 
@@ -614,7 +614,7 @@
     peers = 1 + has[DOWN].astype(jnp.int32) + has[UP].astype(jnp.int32)
     pl.semaphore_wait(barrier, peers)
 
-    def body(c):
+    def body(link_send, c):
         halves = stages[c][1]
         ladder = Ladder(n, units, halves, place, high, link_send, link_recv)
         for u in halves[0] + halves[1]:
@@ -622,7 +622,10 @@
         ladder.run()
         ladder.finish()
 
-    by_core(len(stages), body)
+    def main(link_send):
+        by_core(len(stages), functools.partial(body, link_send))
+
+    pl.run_scoped(main, pltpu.SemaphoreType.DMA((3, n // 2, 2)))
 
 
 def write_rest_kernel(n, kinds, cut, rows, partial, mid, high, result, sems):
@@ -673,7 +676,6 @@
         jax.ShapeDtypeStruct((n * max(size, TILE), wide), jnp.bfloat16)
         for size in (cut[0], cut[1] - cut[0], rows - cut[1])
     )
-    links = [dma((3, depth, 2)), dma((3, depth, 2))]
     gathered = pl.pallas_call(
         functools.partial(gather_kernel, n, width, chunks, units, stages, cut),
         out_shape=[low, serving[1], serving[2], mid, *whole, *column]
@@ -686,16 +688,12 @@
             pltpu.VMEM((2, 1, piece), jnp.float32),
             pltpu.VMEM((3, units[0][2], extents[units[0][0]]), jnp.float32),
             dma((3,)),
-            dma((3,)),
             dma(()),
             dma((len(chunks),)),
             dma((3,)),
-            dma((3,)),
             dma(()),
             dma(()),
-            dma(()),
-            dma(()),
-            *links,
+            dma((3, depth, 2)),
         ],
         compiler_params=pltpu.CompilerParams(
             collective_id=0, has_side_effects=True, vmem_limit_bytes=16 * 1024 * 1024
@@ -721,7 +719,7 @@
         out_shape=[mid, high],
         in_specs=[vmem],
         out_specs=[vmem] * 2,
-        scratch_shapes=links,
+        scratch_shapes=[dma((3, depth, 2))],
         compiler_params=pltpu.CompilerParams(
             collective_id=1, has_side_effects=True, vmem_limit_bytes=16 * 1024 * 1024
         ),

time: 131 us -> 131 us (level)
  no operation moved by 1% of the time
where the time goes in v6:
time: 131 us
  Pallas kernels  130 us (99%)
    pallas_call x1, Pallas kernels, local(): pl.pallas_call(functools.partial(gather_kernel, n, width, chunks, units,...  102 us
    pallas_call x1, Pallas kernels, local(): pl.pallas_call(functools.partial(gather_rest_kernel, n, units, stages, cu...  22 us
    pallas_call x1, Pallas kernels, local(): pl.pallas_call(functools.partial(write_first_kernel, n, kinds, cut), out_...  4.96 us

profile of v6, /device:TPU:0, one launch (start us, length us, event | category | flops | bytes accessed | tf_op | source)
XLA Modules:
  0.0 130.8 jit_solution(15248968039801514592)
XLA Ops:
  0.6 101.8 %shard_map.186 = (bf16[2048,1024]{1,0:T(8,128)(2,1)S(1)}, bf16[4096,256]{1,0:T(8,128)(2,1)S(1)}, bf16[4096,256]{1,0:T(8,128)(2,1)S(1)}, bf16[1024,1024]{1,0:T(8,...) custom-call(f32[512,1024]{1,0:T(8,128)} %w_q.1, ...), custom_call_target="tpu_custom_call" | custom-call | tf_op jit(solution)/shard_map/pallas_call | solution.py:679
  102.5 5.0 %shard_map.187 = (bf16[4096,1024]{1,0:T(8,128)(2,1)}, bf16[4096,256]{1,0:T(8,128)(2,1)}, bf16[4096,256]{1,0:T(8,128)(2,1)}, f32[512,1024]{1,0:T(8,128)}, f32[512...) custom-call(bf16[2048,1024]{1,0:T(8,128)(2,1)S(1)} %get-tuple-elemen, ...), custom_call_target="tpu_custom_call" | custom-call | tf_op jit(solution)/shard_map/pallas_call | solution.py:707
  107.4 22.0 %shard_map.188 = (bf16[1024,1024]{1,0:T(8,128)(2,1)S(1)}, bf16[1024,1024]{1,0:T(8,128)(2,1)S(1)}) custom-call(bf16[256,1024]{1,0:T(8,128)(2,1)S(1)} %get-tuple-element.46.own), custom_call_target="tpu_custom_call" | custom-call | tf_op jit(solution)/shard_map/pallas_call | solution.py:717
  129.4 1.3 %shard_map.189 = bf16[4096,1024]{1,0:T(8,128)(2,1)} custom-call(bf16[4096,1024]{1,0:T(8,128)(2,1)} %get-tuple-element.45.partial, bf16[1024,1024]{1,0:T(8,128)(2,1)S(1)} %get-tuple-element.47.mid, bf16[1024,1024]{1,0:T(8,128)(2,1)S(1)} %get-tuple-element.48.high), custom_call_target="tpu_custom_call", output_to_operand_aliasing={{}: (0, {})} | custom-call | tf_op jit(solution)/shard_map/pallas_call | solution.py:727

commit v7 on v5

--- a/solution.py
+++ b/solution.py
@@ -63,6 +63,8 @@
         self.z, self.x = z, x = lax.div(me, 2), lax.rem(me, 2)
         self.last = last = self.depth - 1
         self.targets = (lax.max(z - 1, 0) * 2 + x, lax.min(z + 1, last) * 2 + x, z * 2 + 1 - x)
+        ends = (z == 0) | (z == last)
+        self.hot_out, self.hot_in = (z == 1, z == last - 1, ends), (z == 0, z == last, ends)
         self.low_end, self.high_end = z <= self.depth // 2 - 2, z >= self.depth // 2 + 1
 
     def joint(self, ref, send_sem, recv_sem):
@@ -75,11 +77,29 @@
             device_id_type=MESH,
         )
 
-    def bundle(self, g, way, slot):
-        there = [u for u in self.halves[g] if not (self.early and u == 0 and isinstance(slot, int) and slot == 0)]
-        words = sum(self.units[u][2] * self.place(u, 0)[0].shape[1] for u in there)
+    def bundle(self, g, way, slot, without=()):
+        words = sum(self.units[u][2] * self.place(u, 0)[0].shape[1] for u in self.halves[g] if u not in without)
         ref = self.spare.at[pl.ds(0, words // self.spare.shape[1])]
         return self.joint(ref, self.link_send.at[way, slot, g], self.link_recv.at[way, slot, g])
+
+    def arrive(self, g, way, slot):
+        self.complete(g, way, slot, self.hot_in[way], lambda copy: copy.wait_recv())
+
+    def leave(self, g, way, slot):
+        self.complete(g, way, slot, self.hot_out[way], lambda copy: copy.wait_send())
+
+    def complete(self, g, way, slot, hot, wait):
+        if self.early and g == 0 and isinstance(slot, int) and slot == 0:
+
+            @pl.when(hot)
+            def _():
+                wait(self.bundle(g, way, slot, (0,)))
+
+            @pl.when(jnp.logical_not(hot))
+            def _():
+                wait(self.bundle(g, way, slot))
+        else:
+            wait(self.bundle(g, way, slot))
 
     def send_unit(self, owner_z, column, u, way, slot):
         ref, at = self.place(u, owner_z * 2 + column)
@@ -99,17 +119,12 @@
             self.send_unit(owner_z, column, u, way, slot)
 
     def send_own(self, u):
-        z, x = self.z, self.x
-
-        @pl.when(z >= 1)
-        def _():
-            self.send_unit(z, x, u, DOWN, 0)
-
-        @pl.when(z <= self.last - 1)
-        def _():
-            self.send_unit(z, x, u, UP, 0)
-
-        self.send_unit(z, x, u, CROSS, 0)
+        has = (self.z >= 1, self.z <= self.last - 1, self.z >= 0)
+        for way in range(3):
+            wanted = has[way]
+            if self.early and u == 0:
+                wanted = wanted & jnp.logical_not(self.hot_out[way])
+            pl.when(wanted)(functools.partial(self.send_unit, self.z, self.x, u, way, 0))
 
     def crosses(self, source, g):
         z, depth, last = self.z, self.depth, self.last
@@ -144,8 +159,8 @@
 
             @pl.when(z + t <= last)
             def _(g=g, before=before):
-                before(DOWN, (z + t) * 2 + x)
-                self.bundle(g, DOWN, t - 1).wait_recv()
+                pl.when(self.hot_in[DOWN])(functools.partial(before, DOWN, (z + t) * 2 + x))
+                self.arrive(g, DOWN, t - 1)
 
                 @pl.when(z >= 1)
                 def _():
@@ -155,8 +170,8 @@
 
             @pl.when(z - t >= 0)
             def _(g=g, before=before):
-                before(UP, (z - t) * 2 + x)
-                self.bundle(g, UP, t - 1).wait_recv()
+                pl.when(self.hot_in[UP])(functools.partial(before, UP, (z - t) * 2 + x))
+                self.arrive(g, UP, t - 1)
 
                 @pl.when(z <= depth - 2)
                 def _():
@@ -166,11 +181,11 @@
 
             if not isinstance(t, int):
                 continue
-            before(CROSS, z * 2 + 1 - x)
+            pl.when(self.hot_in[CROSS])(functools.partial(before, CROSS, z * 2 + 1 - x))
 
             @pl.when(self.low_end | self.high_end)
             def _(g=g):
-                self.bundle(g, CROSS, 0).wait_recv()
+                self.arrive(g, CROSS, 0)
 
                 @pl.when(self.low_end)
                 def _():
@@ -182,12 +197,12 @@
 
         @pl.when((t == last) & (z == 1))
         def _():
-            self.bundle(1, CROSS, depth - 2).wait_recv()
+            self.arrive(1, CROSS, depth - 2)
             self.send(last, 1 - x, 1, DOWN, last)
 
         @pl.when((t == last) & (z == depth - 2))
         def _():
-            self.bundle(1, CROSS, 2).wait_recv()
+            self.arrive(1, CROSS, 2)
             self.send(0, 1 - x, 1, UP, last)
 
         return carry
@@ -211,11 +226,11 @@
 
                 @pl.when((above <= last) & (z >= 1))
                 def _(g=g):
-                    self.bundle(g, DOWN, t).wait_send()
+                    self.leave(g, DOWN, t)
 
                 @pl.when((below >= 0) & (z <= depth - 2))
                 def _(g=g):
-                    self.bundle(g, UP, t).wait_send()
+                    self.leave(g, UP, t)
 
                 both = [(above, t, above <= last)]
                 if not isinstance(t, int):
@@ -224,11 +239,11 @@
 
                     @pl.when(there & self.crosses(source, g))
                     def _(g=g, slot=slot):
-                        self.bundle(g, CROSS, slot).wait_send()
+                        self.leave(g, CROSS, slot)
 
                     @pl.when(there & owed(source, g))
                     def _(g=g, slot=slot):
-                        self.bundle(g, CROSS, slot).wait_recv()
+                        self.arrive(g, CROSS, slot)
 
             return carry
 
@@ -244,19 +259,19 @@
 
             @pl.when(to_above)
             def _(g=g):
-                self.bundle(g, UP, last).wait_send()
+                self.leave(g, UP, last)
 
             @pl.when(to_below)
             def _(g=g):
-                self.bundle(g, DOWN, last).wait_send()
+                self.leave(g, DOWN, last)
 
             @pl.when(from_above)
             def _(g=g):
-                self.bundle(g, DOWN, last).wait_recv()
+                self.arrive(g, DOWN, last)
 
             @pl.when(from_below)
             def _(g=g):
-                self.bundle(g, UP, last).wait_recv()
+                self.arrive(g, UP, last)
 
 
 def by_core(count, body):
@@ -379,7 +394,7 @@
     z, x = lax.div(me, 2), lax.rem(me, 2)
     last = n // 2 - 1
     targets = (lax.max(z - 1, 0) * 2 + x, lax.min(z + 1, last) * 2 + x, z * 2 + 1 - x)
-    has = (z >= 1, z <= last - 1, z >= 0)
+    hot = (z == 1, z == last - 1, (z == 0) | (z == last))
 
     def early(way):
         return pltpu.make_async_remote_copy(
@@ -436,7 +451,7 @@
             copy.start()
         if i == order[min(1, len(order) - 1)]:
             for way in range(3):
-                pl.when(has[way])(lambda way=way: early(way).start())
+                pl.when(hot[way])(lambda way=way: early(way).start())
         if i == first:
             pltpu.make_async_copy(in_norm, in_norm, norm_sem).wait()
             norm_out[me, me_w] = in_norm[0] + in_norm[1]
@@ -475,12 +490,8 @@
                 owner, at, size = units[u]
                 if owner == i:
                     ref, there = place(u, me)
-                    if u > 0:
-                        scaled(wholes[i], at, ref, there, size, factor)
-                        ladder.send_own(u)
-            if i == first:
-                ref, there = place(0, me)
-                scaled(wholes[i], 0, ref, there, units[0][2], factor)
+                    scaled(wholes[i], at, ref, there, size, factor)
+                    ladder.send_own(u)
         ladder.joint(norm_out.at[0, pl.ds(0, width - 1)], wid_send, wid_recv).wait_recv()
         for k in range(1, n):
             pltpu.make_async_remote_copy(
@@ -497,7 +508,7 @@
             ladder.joint(sums[i].at[pl.ds(0, n - 1)], sum_send.at[i], sum_recv.at[i]).wait_send()
         ladder.joint(norm_out.at[pl.ds(0, n - 1)], nrm_send, nrm_recv).wait()
         for way in range(3):
-            pl.when(has[way])(lambda way=way: early(way).wait_send())
+            pl.when(hot[way])(lambda way=way: early(way).wait_send())
         ladder.finish()
 
     by_core(len(stages), body)

time: 131 us -> 131 us (level)
  no operation moved by 1% of the time
where the time goes in v7:
time: 131 us
  Pallas kernels  130 us (99%)
    pallas_call x1, Pallas kernels, local(): pl.pallas_call(functools.partial(gather_kernel, n, width, chunks, units,...  102 us
    pallas_call x1, Pallas kernels, local(): pl.pallas_call(functools.partial(gather_rest_kernel, n, units, stages, cu...  22.3 us
    pallas_call x1, Pallas kernels, local(): pl.pallas_call(functools.partial(write_first_kernel, n, kinds, cut), out_...  4.96 us

profile of v7, /device:TPU:0, one launch (start us, length us, event | category | flops | bytes accessed | tf_op | source)
XLA Modules:
  0.0 130.9 jit_solution(10234489901160431876)
XLA Ops:
  0.6 101.6 %shard_map.186 = (bf16[2048,1024]{1,0:T(8,128)(2,1)S(1)}, bf16[4096,256]{1,0:T(8,128)(2,1)S(1)}, bf16[4096,256]{1,0:T(8,128)(2,1)S(1)}, bf16[1024,1024]{1,0:T(8,...) custom-call(f32[512,1024]{1,0:T(8,128)} %w_q.1, ...), custom_call_target="tpu_custom_call" | custom-call | tf_op jit(solution)/shard_map/pallas_call | solution.py:688
  102.2 5.0 %shard_map.187 = (bf16[4096,1024]{1,0:T(8,128)(2,1)}, bf16[4096,256]{1,0:T(8,128)(2,1)}, bf16[4096,256]{1,0:T(8,128)(2,1)}, f32[512,1024]{1,0:T(8,128)}, f32[512...) custom-call(bf16[2048,1024]{1,0:T(8,128)(2,1)S(1)} %get-tuple-elemen, ...), custom_call_target="tpu_custom_call" | custom-call | tf_op jit(solution)/shard_map/pallas_call | solution.py:720
  107.2 22.3 %shard_map.188 = (bf16[1024,1024]{1,0:T(8,128)(2,1)S(1)}, bf16[1024,1024]{1,0:T(8,128)(2,1)S(1)}) custom-call(bf16[256,1024]{1,0:T(8,128)(2,1)S(1)} %get-tuple-element.46.own), custom_call_target="tpu_custom_call" | custom-call | tf_op jit(solution)/shard_map/pallas_call | solution.py:730
  129.5 1.3 %shard_map.189 = bf16[4096,1024]{1,0:T(8,128)(2,1)} custom-call(bf16[4096,1024]{1,0:T(8,128)(2,1)} %get-tuple-element.45.partial, bf16[1024,1024]{1,0:T(8,128)(2,1)S(1)} %get-tuple-element.47.mid, bf16[1024,1024]{1,0:T(8,128)(2,1)S(1)} %get-tuple-element.48.high), custom_call_target="tpu_custom_call", output_to_operand_aliasing={{}: (0, {})} | custom-call | tf_op jit(solution)/shard_map/pallas_call | solution.py:740
